TPU v7x, 16 devices: a 4x2x1 block of a 4x4x8 slice. The times are simulated.
16 devices in a mesh: dp: 2 (over y, z), fsdp: 8 (over x, core).
Axes of the slice: x: 4, y: 2, z: 1, core: 2. Of those that a mesh axis runs over, the one named last changes fastest.
The devices are a block of a 4x4x8 slice.
Arguments:
- hidden: bfloat16 [16, 1024, 2048], P(('dp', 'fsdp')), parts along dimension 0
- doc_lens: int32 [16], P(('dp', 'fsdp')), parts along dimension 0
- ln_par: float32 [2, 4, 2048], P(None, None, 'fsdp')
- w_qkv: bfloat16 [2, 2048, 8, 768], P(None, 'fsdp')
- b_qkv: bfloat16 [2, 6144], P(None, 'fsdp')
- w_out: bfloat16 [2, 2048, 2048], P(None, 'fsdp')
- b_out: bfloat16 [2, 2048], P(None, 'fsdp')
- w_up: bfloat16 [2, 2048, 8192], P(None, 'fsdp')
- b_up: bfloat16 [2, 8192], P(None, 'fsdp')
- w_down: bfloat16 [2, 8192, 2048], P(None, 'fsdp')
- b_down: bfloat16 [2, 2048], P(None, 'fsdp')
Outputs:
- output: bfloat16 [16, 1024, 2048], P(('dp', 'fsdp')), parts along dimension 0
There are 2 independent parts. A program takes and returns all parts, laid end to end along the dimension named above; an argument that names none is the same for every part.
All inputs are finite; a program needn't handle non-finite values.
Results may differ from a plain program's by a relative error of at most 0.0071295.
Values are sent between devices in bfloat16 or wider.
A program may use at most 768 MiB of HBM per device.

v0:
```python
import jax
import jax.numpy as jnp
from jax import lax
from jax.sharding import PartitionSpec as P

ROPE_BASE = 10000.0
LN_EPS = 1e-5


def layer_norm(row_vals, gain_vec, shift_vec):
    mean_vals = jnp.mean(row_vals, axis=-1, keepdims=True)
    centered = row_vals - mean_vals
    var_vals = jnp.mean(centered * centered, axis=-1, keepdims=True)
    normed = centered * lax.rsqrt(var_vals + LN_EPS)
    return (normed * gain_vec + shift_vec).astype(jnp.bfloat16)


def rotary_tables(seq_len, rot_dim):
    inv_freq = 1.0 / (ROPE_BASE ** (jnp.arange(0, rot_dim, 2, dtype=jnp.float32) / rot_dim))
    angles = jnp.arange(seq_len, dtype=jnp.float32)[:, None] * inv_freq[None, :]
    angles = jnp.concatenate([angles, angles], axis=-1)
    return jnp.cos(angles), jnp.sin(angles)


def apply_rotary(head_vals, cos_tab, sin_tab):
    rot_dim = cos_tab.shape[-1]
    half_rot = rot_dim // 2
    rot_part = head_vals[..., :rot_dim].astype(jnp.float32)
    turned = jnp.concatenate([-rot_part[..., half_rot:], rot_part[..., :half_rot]], axis=-1)
    rotated = rot_part * cos_tab[:, None, :] + turned * sin_tab[:, None, :]
    return jnp.concatenate([rotated.astype(jnp.bfloat16), head_vals[..., rot_dim:]], axis=-1)


def attention_core(qkv_heads, lens_loc):
    num_docs, seq_len, num_heads, triple = qkv_heads.shape
    head_dim = triple // 3
    cos_tab, sin_tab = rotary_tables(seq_len, head_dim // 4)
    queries = apply_rotary(qkv_heads[..., :head_dim], cos_tab, sin_tab)
    keys_rot = apply_rotary(qkv_heads[..., head_dim:2 * head_dim], cos_tab, sin_tab)
    values = qkv_heads[..., 2 * head_dim:]
    scores = jnp.einsum('nqhe,nkhe->nhqk', queries, keys_rot, preferred_element_type=jnp.float32) * (head_dim ** -0.5)
    positions = jnp.arange(seq_len)
    causal = positions[None, :] <= positions[:, None]
    visible = causal[None, None] & (positions[None, None, None, :] < lens_loc[:, None, None, None])
    prob_bf = jax.nn.softmax(jnp.where(visible, scores, -1e30), axis=-1).astype(jnp.bfloat16)
    context = jnp.einsum('nhqk,nkhe->nqhe', prob_bf, values, preferred_element_type=jnp.float32)
    return context.astype(jnp.bfloat16).reshape(num_docs * seq_len, num_heads * head_dim)


def layer_forward(x_loc, lens_loc, ln_full, w_qkv_full, b_qkv_full, w_out_full, b_out_full, w_up_full, b_up_full, w_down_full, b_down_full):
    num_docs, seq_len, d_model = x_loc.shape
    x_rows = x_loc.reshape(num_docs * seq_len, d_model).astype(jnp.float32)
    attn_in = layer_norm(x_rows, ln_full[0], ln_full[1])
    mlp_in = layer_norm(x_rows, ln_full[2], ln_full[3])
    qkv_rows = jnp.dot(attn_in, w_qkv_full.reshape(d_model, -1), preferred_element_type=jnp.float32) + b_qkv_full.astype(jnp.float32)
    qkv_heads = qkv_rows.astype(jnp.bfloat16).reshape(num_docs, seq_len, w_qkv_full.shape[1], w_qkv_full.shape[2])
    context = attention_core(qkv_heads, lens_loc)
    attn_out = jnp.dot(context, w_out_full, preferred_element_type=jnp.float32) + b_out_full.astype(jnp.float32)
    up_rows = jnp.dot(mlp_in, w_up_full, preferred_element_type=jnp.float32) + b_up_full.astype(jnp.float32)
    act_rows = jax.nn.gelu(up_rows, approximate=False).astype(jnp.bfloat16)
    mlp_out = jnp.dot(act_rows, w_down_full, preferred_element_type=jnp.float32) + b_down_full.astype(jnp.float32)
    return (x_rows + attn_out + mlp_out).astype(jnp.bfloat16).reshape(num_docs, seq_len, d_model)


def gather_full(piece, axis_idx):
    return lax.all_gather(piece, 'fsdp', axis=axis_idx, tiled=True)


def solution(mesh):
    row_spec = P(('dp', 'fsdp'), None, None)
    in_specs = (row_spec, P(('dp', 'fsdp')), P(None, None, 'fsdp'), P(None, 'fsdp', None, None), P(None, 'fsdp'), P(None, 'fsdp', None), P(None, 'fsdp'), P(None, 'fsdp', None), P(None, 'fsdp'), P(None, 'fsdp', None), P(None, 'fsdp'))

    def local_step(hidden_loc, lens_loc, ln_par, w_qkv, b_qkv, w_out, b_out, w_up, b_up, w_down, b_down):
        x_loc = hidden_loc
        for layer_idx in range(ln_par.shape[0]):
            ln_full = gather_full(ln_par[layer_idx], 1)
            w_qkv_full = gather_full(w_qkv[layer_idx], 0)
            b_qkv_full = gather_full(b_qkv[layer_idx], 0)
            w_out_full = gather_full(w_out[layer_idx], 0)
            b_out_full = gather_full(b_out[layer_idx], 0)
            w_up_full = gather_full(w_up[layer_idx], 0)
            b_up_full = gather_full(b_up[layer_idx], 0)
            w_down_full = gather_full(w_down[layer_idx], 0)
            b_down_full = gather_full(b_down[layer_idx], 0)
            x_loc = layer_forward(x_loc, lens_loc, ln_full, w_qkv_full, b_qkv_full, w_out_full, b_out_full, w_up_full, b_up_full, w_down_full, b_down_full)
        return x_loc

    return jax.shard_map(local_step, mesh=mesh, in_specs=in_specs, out_specs=row_spec, check_vma=False)
```

profile of v0, /device:TPU:113, one launch (start us, length us, event | category | flops | bytes accessed | tf_op | source)
XLA Modules:
  0.0 1002.7 jit_solution(8054171844860117068)
XLA Ops:
  29.8 21.7 %all-gather = f32[1,4,2048]{2,1,0:T(4,128)S(1)} all-gather(f32[1,4,256]{2,1,0:T(4,128)S(1)} %get-tuple-element.40), channel_id=2, replica_groups=mesh['dp'=2,'fsdp'=8] {'fsdp'}, dimensions={2}, use_global_device_ids=true | all-gather | bytes 36864 | tf_op jit(solution)/shard_map/all_gather | solution.py:66
  58.4 21.7 %all-gather.2 = bf16[1,6144]{1,0:T(2,128)(2,1)S(1)} all-gather(bf16[1,768]{1,0:T(2,128)(2,1)S(1)} %get-tuple-element.44), channel_id=4, replica_groups=mesh['dp'=2,'fsdp'=8] {'fsdp'}, dimensions={1}, use_global_device_ids=true | all-gather | bytes 13824 | tf_op jit(solution)/shard_map/all_gather | solution.py:66
  84.6 21.5 %all-gather.6 = bf16[1,8192]{1,0:T(2,128)(2,1)S(1)} all-gather(bf16[1,1024]{1,0:T(2,128)(2,1)S(1)} %get-tuple-element.41), channel_id=8, replica_groups=mesh['dp'=2,'fsdp'=8] {'fsdp'}, dimensions={1}, use_global_device_ids=true | all-gather | bytes 18432 | tf_op jit(solution)/shard_map/all_gather | solution.py:66
  106.8 23.1 %all-gather.4 = bf16[1,2048]{1,0:T(2,128)(2,1)S(1)} all-gather(bf16[1,256]{1,0:T(2,128)(2,1)S(1)} %get-tuple-element.46), channel_id=6, replica_groups=mesh['dp'=2,'fsdp'=8] {'fsdp'}, dimensions={1}, use_global_device_ids=true | all-gather | bytes 4608 | tf_op jit(solution)/shard_map/all_gather | solution.py:66
  130.5 19.8 %all-gather.8 = bf16[1,2048]{1,0:T(2,128)(2,1)S(1)} all-gather(bf16[1,256]{1,0:T(2,128)(2,1)S(1)} %get-tuple-element.48), channel_id=10, replica_groups=mesh['dp'=2,'fsdp'=8] {'fsdp'}, dimensions={1}, use_global_device_ids=true | all-gather | bytes 4608 | tf_op jit(solution)/shard_map/all_gather | solution.py:66
  150.9 24.6 %all-gather.9 = f32[1,4,2048]{2,1,0:T(4,128)S(1)} all-gather(f32[1,4,256]{2,1,0:T(4,128)S(1)} %get-tuple-element.39), channel_id=11, replica_groups=mesh['dp'=2,'fsdp'=8] {'fsdp'}, dimensions={2}, use_global_device_ids=true | all-gather | bytes 36864 | tf_op jit(solution)/shard_map/all_gather | solution.py:66
  176.1 21.4 %all-gather.11 = bf16[1,6144]{1,0:T(2,128)(2,1)S(1)} all-gather(bf16[1,768]{1,0:T(2,128)(2,1)S(1)} %get-tuple-element.43), channel_id=13, replica_groups=mesh['dp'=2,'fsdp'=8] {'fsdp'}, dimensions={1}, use_global_device_ids=true | all-gather | bytes 13824 | tf_op jit(solution)/shard_map/all_gather | solution.py:66
  198.2 23.8 %all-gather.15 = bf16[1,8192]{1,0:T(2,128)(2,1)S(1)} all-gather(bf16[1,1024]{1,0:T(2,128)(2,1)S(1)} %get-tuple-element.42), channel_id=17, replica_groups=mesh['dp'=2,'fsdp'=8] {'fsdp'}, dimensions={1}, use_global_device_ids=true | all-gather | bytes 18432 | tf_op jit(solution)/shard_map/all_gather | solution.py:66
  222.6 21.2 %all-gather.13 = bf16[1,2048]{1,0:T(2,128)(2,1)S(1)} all-gather(bf16[1,256]{1,0:T(2,128)(2,1)S(1)} %get-tuple-element.45), channel_id=15, replica_groups=mesh['dp'=2,'fsdp'=8] {'fsdp'}, dimensions={1}, use_global_device_ids=true | all-gather | bytes 4608 | tf_op jit(solution)/shard_map/all_gather | solution.py:66
  244.4 20.9 %all-gather.17 = bf16[1,2048]{1,0:T(2,128)(2,1)S(1)} all-gather(bf16[1,256]{1,0:T(2,128)(2,1)S(1)} %get-tuple-element.47), channel_id=19, replica_groups=mesh['dp'=2,'fsdp'=8] {'fsdp'}, dimensions={1}, use_global_device_ids=true | all-gather | bytes 4608 | tf_op jit(solution)/shard_map/all_gather | solution.py:66
  265.9 24.3 %copy.59 = bf16[256,8,8,768]{3,1,2,0:T(8,128)(2,1)} copy(bf16[256,8,8,768]{3,2,1,0:T(8,128)(2,1)} %bitcast.153) | data formatting | bytes 50331648
  290.2 30.0 %add_convert_fusion.1 = bf16[1024,6144]{1,0:T(8,128)(2,1)S(1)} fusion(f32[6144]{0:T(1024)S(1)} %bitcast.160, bf16[2048,6144]{1,0:T(8,128)(2,1)} %bitcast.155, bf16[1,1024,2048]{2,1,0:T(8,128)(2,1)S(1)} %copy-done.3, f32[2048]{0:T(1024)S(1)} %bitcast.172, f32[2048]{0:T(1024)S(1)} %bitcast.171, f32[1024]{0:T(1024)S(1)} %add_rsqrt_fusion.1, ...), kind=kOutput, calls=%fused_computation.57 | convolution fusion | flops 25794969600 | bytes 41992192 | tf_op jit(solution)/shard_map/dot_general | solution.py:55
  353.8 26.4 %copy.61 = bf16[256,8,8,768]{3,1,2,0:T(8,128)(2,1)} copy(bf16[256,8,8,768]{3,2,1,0:T(8,128)(2,1)} %bitcast.152) | data formatting | bytes 50331648
  384.2 17.6 %fusion.112 = f32[8,1024,1024]{1,2,0:T(8,128)} fusion(bf16[1,1024,8,192]{3,1,2,0:T(8,128)(2,1)} %copy.51, bf16[1,1024,8,64]{3,1,2,0:T(8,128)(2,1)} %get-tuple-element.28, bf16[1,1024,8,192]{3,1,2,0:T(8,128)(2,1)} %copy.53, bf16[1,1024,8,64]{3,1,2,0:T(8,128)(2,1)} %get-tuple-element.27), kind=kOutput, calls=%fused_computation.133 | convolution fusion | flops 4311744512 | bytes 41943040 | tf_op jit(solution)/shard_map/nqhe,nkhe->nhqk/dot_general | solution.py:41
  401.8 33.8 %fusion.243 = (f32[8,1024]{1,0:T(8,128)S(1)}, f32[8,1024,1024]{1,2,0:T(8,128)}) fusion(f32[8,1024,1024]{1,2,0:T(8,128)} %fusion.112, pred[1024,1024]{0,1:T(8,128)(4,1)S(1)} %copy-done.15), kind=kOutput, calls=%fused_computation.271 | output fusion | flops 50332672 | bytes 68190208 | tf_op jit(solution)/shard_map/sub | solution.py:45
  452.1 123.0 %fusion.4.clone.4 = bf16[1024,8192]{1,0:T(8,128)(2,1)} fusion(bf16[1,2048,8192]{2,1,0:T(8,128)(2,1)} %all-gather.31.cloned.1.call-done, f32[8192]{0:T(1024)S(1)} %bitcast.158, bf16[1,1024,2048]{2,1,0:T(8,128)(2,1)} %param.11, f32[2048]{0:T(1024)S(1)} %bitcast.168, f32[2048]{0:T(1024)S(1)} %bitcast.167, f32[1024]{0:T(1024)S(1)} %copy-done.36, ...), kind=kOutput, calls=%fused_computation.6.clone.clone.clone.1 | convolution fusion | flops 34925969408 | bytes 54583296 | tf_op jit(solution)/shard_map/dot_general | solution.py:59
  575.1 43.4 %fusion.12 = f32[1024,2048]{1,0:T(8,128)} fusion(bf16[1,8192,2048]{2,1,0:T(8,128)(2,1)} %all-gather.33.cloned.1.call-done, bf16[1024,8192]{1,0:T(8,128)(2,1)} %fusion.4.clone.4), kind=kOutput, calls=%fused_computation.14 | convolution fusion | flops 34359738368 | bytes 58720256 | tf_op jit(solution)/shard_map/dot_general | solution.py:61
  618.5 17.4 %convert_reduce_fusion = (f32[1024]{0:T(1024)S(1)}, bf16[1024,2048]{1,0:T(8,128)(2,1)S(1)}) fusion(f32[1024,2048]{1,0:T(8,128)} %fusion.12, f32[2048]{0:T(1024)S(1)} %bitcast.164, f32[2048]{0:T(1024)S(1)} %bitcast.163, bf16[1024,2048]{0,1:T(8,128)(2,1)} %bitcast.173, bf16[1,2048,2048]{2,1,0:T(8,128)(2,1)} %all-gather.29.cloned.1.call-done, ...), kind=kOutput, calls=%fused_computation.90 | convolution fusion | flops 8606710784 | bytes 29380608 | tf_op jit(solution)/shard_map/dot_general | solution.py:58
  638.0 31.7 %add_convert_fusion = bf16[1024,6144]{1,0:T(8,128)(2,1)} fusion(f32[6144]{0:T(1024)S(1)} %bitcast.159, bf16[2048,6144]{1,0:T(8,128)(2,1)} %bitcast.154, bf16[1024,2048]{1,0:T(8,128)(2,1)S(1)} %get-tuple-element.52, f32[2048]{0:T(1024)S(1)} %bitcast.170, f32[2048]{0:T(1024)S(1)} %bitcast.169, f32[1024]{0:T(1024)S(1)} %add_rsqrt_fusion, ...), kind=kOutput, calls=%fused_computation.56 | convolution fusion | flops 25794969600 | bytes 41992192 | tf_op jit(solution)/shard_map/dot_general | solution.py:55
  737.5 17.5 %fusion.121 = f32[8,1024,1024]{1,2,0:T(8,128)} fusion(bf16[1,1024,8,192]{3,1,2,0:T(8,128)(2,1)} %copy.56, bf16[1,1024,8,64]{3,1,2,0:T(8,128)(2,1)} %get-tuple-element.26, bf16[1,1024,8,192]{3,1,2,0:T(8,128)(2,1)} %copy.58, bf16[1,1024,8,64]{3,1,2,0:T(8,128)(2,1)} %get-tuple-element.25), kind=kOutput, calls=%fused_computation.146 | convolution fusion | flops 4311744512 | bytes 41943040 | tf_op jit(solution)/shard_map/nqhe,nkhe->nhqk/dot_general | solution.py:41
  769.0 115.4 %fusion.7.clone.4 = bf16[1024,8192]{1,0:T(8,128)(2,1)} fusion(bf16[1,2048,8192]{2,1,0:T(8,128)(2,1)} %all-gather.39.cloned.1.call-done, f32[8192]{0:T(1024)S(1)} %bitcast.157, bf16[1024,2048]{1,0:T(8,128)(2,1)} %copy-done.13, f32[2048]{0:T(1024)S(1)} %bitcast.166, f32[2048]{0:T(1024)S(1)} %bitcast.165, f32[1024]{0:T(1024)S(1)} %add_rsqrt_fusion, ...), kind=kOutput, calls=%fused_computation.9.clone.clone.clone.1 | convolution fusion | flops 34925969408 | bytes 54583296 | tf_op jit(solution)/shard_map/dot_general | solution.py:59
  884.4 33.4 %fusion.244 = (f32[8,1024]{1,0:T(8,128)S(1)}, f32[8,1024,1024]{1,2,0:T(8,128)}) fusion(f32[8,1024,1024]{1,2,0:T(8,128)} %fusion.121, pred[1024,1024]{0,1:T(8,128)(4,1)S(1)} %copy-done.16), kind=kOutput, calls=%fused_computation.272 | output fusion | flops 50332672 | bytes 68190208 | tf_op jit(solution)/shard_map/sub | solution.py:45
  934.1 43.5 %fusion.8 = f32[1024,2048]{1,0:T(8,128)} fusion(bf16[1,8192,2048]{2,1,0:T(8,128)(2,1)} %all-gather.41.cloned.1.call-done, bf16[1024,8192]{1,0:T(8,128)(2,1)} %fusion.7.clone.4), kind=kOutput, calls=%fused_computation.10 | convolution fusion | flops 34359738368 | bytes 58720256 | tf_op jit(solution)/shard_map/dot_general | solution.py:61
  977.6 18.0 %fusion.154 = bf16[1,1024,2048]{2,1,0:T(8,128)(2,1)} fusion(f32[1024,2048]{1,0:T(8,128)} %fusion.8, f32[2048]{0:T(1024)S(1)} %bitcast.162, f32[2048]{0:T(1024)S(1)} %bitcast.161, bf16[1024,2048]{0,1:T(8,128)(2,1)} %bitcast.174, bf16[1,2048,2048]{2,1,0:T(8,128)(2,1)} %all-gather.37.cloned.1.call-done, bf16[1024,2048]{1,0:T(8,128)(2,1)} %copy-done.13), kind=kOutput, calls=%fused_computation.174 | convolution fusion | flops 8602517504 | bytes 29376512 | tf_op jit(solution)/shard_map/dot_general | solution.py:58
  (160 shorter events, 192.7 us)
Async XLA Ops:
  6.5 259.4 %all-gather.27.cloned.1.call-start = ((), (), s32[]{:S(2)}) async-start(), calls=%async_computation | async-start | bytes 28311552 | tf_op jit(solution)/shard_map/all_gather | solution.py:66
  12.6 341.1 %all-gather.35.cloned.1.call-start = ((), (), s32[]{:S(2)}) async-start(), calls=%async_computation.4 | async-start | bytes 28311552 | tf_op jit(solution)/shard_map/all_gather | solution.py:66
  13.4 438.6 %all-gather.31.cloned.1.call-start = ((), (), s32[]{:S(2)}) async-start(), calls=%async_computation.2 | async-start | bytes 37748736 | tf_op jit(solution)/shard_map/all_gather | solution.py:66
  19.5 555.7 %all-gather.33.cloned.1.call-start = ((), (), s32[]{:S(2)}) async-start(), calls=%async_computation.3 | async-start | bytes 37748736 | tf_op jit(solution)/shard_map/all_gather | solution.py:66
  25.9 592.6 %all-gather.29.cloned.1.call-start = ((), (), s32[]{:S(2)}) async-start(), calls=%async_computation.1 | async-start | bytes 9437184 | tf_op jit(solution)/shard_map/all_gather | solution.py:66
  27.5 741.5 %all-gather.39.cloned.1.call-start = ((), (), s32[]{:S(2)}) async-start(), calls=%async_computation.6 | async-start | bytes 37748736 | tf_op jit(solution)/shard_map/all_gather | solution.py:66
  27.6 30.8 %copy-start.23 = (bf16[2,768]{1,0:T(2,128)(2,1)S(1)}, bf16[2,768]{1,0:T(2,128)(2,1)}, u32[]{:S(2)}) copy-start(bf16[2,768]{1,0:T(2,128)(2,1)} %param.15) | copy-start | bytes 9220
  28.2 906.0 %all-gather.41.cloned.1.call-start = ((), (), s32[]{:S(2)}) async-start(), calls=%async_computation.7 | async-start | bytes 37748736 | tf_op jit(solution)/shard_map/all_gather | solution.py:66
  28.2 56.4 %copy-start.20 = (bf16[2,1024]{1,0:T(2,128)(2,1)S(1)}, bf16[2,1024]{1,0:T(2,128)(2,1)}, u32[]{:S(2)}) copy-start(bf16[2,1024]{1,0:T(2,128)(2,1)} %param.19) | copy-start | bytes 12292
  28.2 78.5 %copy-start.37 = (bf16[2,256]{1,0:T(2,128)(2,1)S(1)}, bf16[2,256]{1,0:T(2,128)(2,1)}, u32[]{:S(2)}) copy-start(bf16[2,256]{1,0:T(2,128)(2,1)} %param.17) | copy-start | bytes 3076
  28.3 102.2 %copy-start.38 = (bf16[2,256]{1,0:T(2,128)(2,1)S(1)}, bf16[2,256]{1,0:T(2,128)(2,1)}, u32[]{:S(2)}) copy-start(bf16[2,256]{1,0:T(2,128)(2,1)} %param.21) | copy-start | bytes 3076
  29.0 948.7 %all-gather.37.cloned.1.call-start = ((), (), s32[]{:S(2)}) async-start(), calls=%async_computation.5 | async-start | bytes 9437184 | tf_op jit(solution)/shard_map/all_gather | solution.py:66
  54.9 235.3 %copy-start.21 = (f32[1024]{0:T(1024)}, f32[1024]{0:T(1024)S(1)}, u32[]{:S(2)}) copy-start(f32[1024]{0:T(1024)S(1)} %broadcast_multiply_fusion.1) | copy-start | bytes 12292
  58.4 231.8 %copy-start.35 = (f32[1024]{0:T(1024)}, f32[1024]{0:T(1024)S(1)}, u32[]{:S(2)}) copy-start(f32[1024]{0:T(1024)S(1)} %add_rsqrt_fusion.1) | copy-start | bytes 12292
  82.6 297.6 %copy-start.9 = (f32[1024,64]{1,0:T(8,128)}, f32[1024,64]{1,0:T(8,128)S(1)}, u32[]{:S(2)}) copy-start(f32[1024,64]{1,0:T(8,128)S(1)} %get-tuple-element.29) | copy-start | bytes 786436
  82.6 297.6 %copy-start.11 = (f32[1024,64]{1,0:T(8,128)}, f32[1024,64]{1,0:T(8,128)S(1)}, u32[]{:S(2)}) copy-start(f32[1024,64]{1,0:T(8,128)S(1)} %get-tuple-element.30) | copy-start | bytes 786436
  575.1 43.4 %copy-start.27 = (f32[1,2048]{1,0:T(1,128)S(1)}, f32[1,2048]{1,0:T(1,128)}, u32[]{:S(2)}) copy-start(f32[1,2048]{1,0:T(1,128)} %convert_element_type.156) | copy-start | bytes 24580
  575.1 43.4 %copy-start.28 = (f32[1,2048]{1,0:T(1,128)S(1)}, f32[1,2048]{1,0:T(1,128)}, u32[]{:S(2)}) copy-start(f32[1,2048]{1,0:T(1,128)} %convert_element_type.158) | copy-start | bytes 24580
  737.5 31.5 %copy-start.17 = (f32[1,8192]{1,0:T(1,128)S(1)}, f32[1,8192]{1,0:T(1,128)}, u32[]{:S(2)}) copy-start(f32[1,8192]{1,0:T(1,128)} %convert_element_type.161) | copy-start | bytes 98308
  737.5 31.5 %copy-start.29 = (f32[1,1,2048]{2,1,0:T(1,128)S(1)}, f32[1,1,2048]{2,1,0:T(1,128)}, u32[]{:S(2)}) copy-start(f32[1,1,2048]{2,1,0:T(1,128)} %get-tuple-element.32) | copy-start | bytes 24580
  737.5 31.5 %copy-start.30 = (f32[1,1,2048]{2,1,0:T(1,128)S(1)}, f32[1,1,2048]{2,1,0:T(1,128)}, u32[]{:S(2)}) copy-start(f32[1,1,2048]{2,1,0:T(1,128)} %get-tuple-element.34) | copy-start | bytes 24580
  769.0 115.4 %copy-start.16 = (pred[1024,1024]{0,1:T(8,128)(4,1)S(1)}, pred[1024,1024]{0,1:T(8,128)(4,1)}, u32[]{:S(2)}) copy-start(pred[1024,1024]{0,1:T(8,128)(4,1)} %fusion.153) | copy-start | bytes 3145732
  934.1 43.5 %copy-start.25 = (f32[1,2048]{1,0:T(1,128)S(1)}, f32[1,2048]{1,0:T(1,128)}, u32[]{:S(2)}) copy-start(f32[1,2048]{1,0:T(1,128)} %convert_element_type.160) | copy-start | bytes 24580
  934.1 43.5 %copy-start.26 = (f32[1,2048]{1,0:T(1,128)S(1)}, f32[1,2048]{1,0:T(1,128)}, u32[]{:S(2)}) copy-start(f32[1,2048]{1,0:T(1,128)} %convert_element_type.162) | copy-start | bytes 24580
  (23 other events, 371.3 us)
Sparse Core Ops, SparseCore 0:
  12.8 122.2 all-gather.26
  136.6 119.8 all-gather.34
  258.1 153.5 all-gather.30
  413.2 153.5 all-gather.32
  568.2 46.3 all-gather.28
  616.1 152.8 all-gather.38
  770.6 153.5 all-gather.40
  925.8 46.3 all-gather.36
where the time goes:
time: 1010 us; the launch traced here: 1000 us
  matrix products  490 us (49%)
  blocking collectives  220 us (22%)
  local copies, waits for them, and re-layouts  143 us (14%)
  other arithmetic  117 us (12%)
  waiting for transfers between devices  16.9 us (2%)
  between operations  14.9 us (1%)
    dot_general x2, matrix products, layer_forward(): jnp.dot(mlp_in, w_up_full, preferred_element_type=jnp.float32)  238 us
    all_gather x10, blocking collectives, gather_full(): return lax.all_gather(piece, 'fsdp', axis=axis_idx, tiled=True)  220 us
    unnamed x89, local copies, waits for them, and re-layouts  90.5 us
    dot_general x2, matrix products, layer_forward(): jnp.dot(act_rows, w_down_full, preferred_element_type=jnp.float32)  86.9 us
    sub x2, other arithmetic, attention_core(): jax.nn.softmax(jnp.where(visible, scores, -1e+30), axis=-1)  67.2 us
    dot_general x2, matrix products, layer_forward(): jnp.dot(attn_in, w_qkv_full.reshape(d_model, -1), preferred_element_type=...  61.7 us
    dot_general x2, matrix products, layer_forward(): jnp.dot(context, w_out_full, preferred_element_type=jnp.float32)  35.4 us
    dot_general x2, matrix products, attention_core(): jnp.einsum('nqhe,nkhe->nhqk', queries, keys_rot, preferred_element_type=j...  35.1 us
  transfers between devices with their start and end apart: 8, of which 1 were waited for; matrix products, arithmetic and copies ran while one was open for 72% of the time, Pallas kernels for 0%

commit v1 on v0

v1 whole, which is shorter than its diff:
```python
import functools

import jax
import jax.numpy as jnp
from jax import lax
from jax.experimental import pallas as pl
from jax.experimental.pallas import tpu as pltpu
from jax.sharding import PartitionSpec as P

ROPE_BASE = 10000.0
LN_EPS = 1e-5
MESH = pl.DeviceIdType.MESH
SLOTS = 16
LAG = 6
ROWS = 256
F32 = jnp.float32
BF16 = jnp.bfloat16


def rope_tables(seq_len, rot_dim, width):
    half = rot_dim // 2
    inv_freq = 1.0 / (ROPE_BASE ** (jnp.arange(0, rot_dim, 2, dtype=F32) / rot_dim))
    angles = jnp.arange(seq_len, dtype=F32)[:, None] * inv_freq[None, :]
    cos, sin = jnp.cos(angles), jnp.sin(angles)
    rest = width - rot_dim
    one, zero = jnp.ones((seq_len, rest), F32), jnp.zeros((seq_len, rest), F32)
    none = jnp.zeros((seq_len, half), F32)
    keep = jnp.concatenate([cos, cos, one], axis=1)
    low = jnp.concatenate([-sin, none, zero], axis=1)
    high = jnp.concatenate([none, sin, zero], axis=1)
    return jnp.stack([keep, low, high])


def kernel(dims, hid, lens, small, tabs, wq, wo, wu, wd, out, gath, xs, a_s, m_s, ctx, act, acc, q_s, k_s, v_s, wbuf,
           smallg, send, cw, ccw, ysem, dd, ld, small_send, small_recv, io_sem):
    n, num_layers, heads, tile, seq, d_model, rps, rot_half = dims
    ring = n // 2
    n_a, n_b, n_c = heads, n * rps // 2, d_model // tile
    per_layer = n_a + n_b + n_c
    chunks = num_layers * per_layer
    wide = tabs.shape[2]
    scale = float(tile) ** -0.5

    d, f = lax.axis_index("dp"), lax.axis_index("fsdp")
    x, c = f // 2, f % 2
    par = d % 2
    right = ((x + 1) % ring) * 2 + c
    left = ((x + ring - 1) % ring) * 2 + c
    sib = x * 2 + 1 - c
    mate = d + 1 - 2 * par
    mine, other = 2 * par, 2 - 2 * par

    def remote(src, dst, s_sem, r_sem, where):
        return pltpu.make_async_remote_copy(
            src_ref=src, dst_ref=dst, send_sem=s_sem, recv_sem=r_sem, device_id=where, device_id_type=MESH)

    to_right, to_left, to_sib, to_mate = {"fsdp": right}, {"fsdp": left}, {"fsdp": sib}, {"dp": mate}

    def q_tile(l, r, i):
        return wq.at[l, :, pl.ds(pl.multiple_of(r * (3 * tile) + i * tile, tile), tile)]

    def up_tile(l, u):
        return wu.at[l, :, pl.ds(pl.multiple_of((u % n) * (rps * tile) + (u // n) * tile, tile), tile)]

    def down_tile(l, v):
        return wd.at[l, pl.ds(pl.multiple_of((v // n_c) * tile, tile), tile),
                     pl.ds(pl.multiple_of((v % n_c) * tile, tile), tile)]

    def out_tile(l, j):
        return wo.at[l, :, pl.ds(pl.multiple_of(j * tile, tile), tile)]

    def send_own(k):
        slot = k % SLOTS
        l, r = k // per_layer, k % per_layer

        def go(own):
            remote(own(mine), gath.at[k, mine, f], send.at[slot], cw.at[slot, 0], to_right).start()
            remote(own(1), gath.at[k, 1, f], send.at[slot], ccw.at[slot, 0], to_left).start()
            for i in range(3):
                remote(own(i), gath.at[k, i, f], send.at[slot], dd.at[slot], to_sib).start()

        @pl.when(r < n_a)
        def _():
            go(lambda i: q_tile(l, r, i))

        @pl.when((r >= n_a) & (r < n_a + n_b))
        def _():
            j = r - n_a
            go(lambda i: down_tile(l, j) if isinstance(i, int) and i == 1 else up_tile(l, 2 * j + i // 2))

        @pl.when(r >= n_a + n_b)
        def _():
            j = r - n_a - n_b
            go(lambda i: out_tile(l, j) if isinstance(i, int) and i == 1 else down_tile(l, n_b + 2 * j + i // 2))

    def from_left(hop):
        return ((x + ring - hop) % ring) * 2 + c

    def from_right(hop):
        return ((x + hop) % ring) * 2 + c

    def wait_tile(sem):
        ref = gath.at[0, 0, 0]
        pltpu.make_async_copy(ref, ref, sem).wait()

    def pass_on(k, hop):
        slot = k % SLOTS
        fx, fy = from_left(hop), from_right(hop)
        wait_tile(cw.at[slot, hop - 1])
        t_cw = gath.at[k, mine, fx]
        if hop < ring - 1:
            remote(t_cw, t_cw, send.at[slot], cw.at[slot, hop], to_right).start()
        remote(t_cw, t_cw, send.at[slot], ysem.at[slot, hop - 1], to_mate).start()
        remote(t_cw, t_cw, send.at[slot], dd.at[slot], to_sib).start()
        wait_tile(ccw.at[slot, hop - 1])
        t_ccw = gath.at[k, 1, fy]
        if hop < ring - 1:
            remote(t_ccw, t_ccw, send.at[slot], ccw.at[slot, hop], to_left).start()
        remote(t_ccw, t_ccw, send.at[slot], dd.at[slot], to_sib).start()

    def pass_mate(k, hop):
        slot = k % SLOTS
        wait_tile(ysem.at[slot, hop - 1])
        t_y = gath.at[k, other, from_left(hop)]
        remote(t_y, t_y, send.at[slot], dd.at[slot], to_sib).start()

    sib_tiles = 3 * ring
    sent_tiles = 2 * (ring - 1) + (ring - 1) + sib_tiles

    def wait_sib(k):
        ref = gath.at[0, :, pl.ds(0, sib_tiles // 3)]
        pltpu.make_async_copy(ref, ref, dd.at[k % SLOTS]).wait()

    def wait_sent(k):
        ref = gath.at[0, :, pl.ds(0, sent_tiles // 3)]
        pltpu.make_async_copy(ref, ref, send.at[k % SLOTS]).wait()

    def load_tile(k, i, to, own):
        slot = k % 2
        kk = k if to < 3 else k - 4
        for step in range(1, n):
            s = (f + step) % n
            pltpu.make_async_copy(
                gath.at[kk, i, s], wbuf.at[slot, to, pl.ds(pl.multiple_of(s * tile, tile), tile)], ld.at[slot, to]).start()
        pltpu.make_async_copy(own, wbuf.at[slot, to, pl.ds(pl.multiple_of(f * tile, tile), tile)], ld.at[slot, to]).start()

    def load(k):
        l, r = k // per_layer, k % per_layer

        @pl.when(r < n_a)
        def _():
            for i in range(3):
                load_tile(k, i, i, q_tile(l, r, i))

        @pl.when((r >= n_a) & (r < n_a + n_b))
        def _():
            for i in (0, 2):
                load_tile(k, i, i, up_tile(l, 2 * (r - n_a) + i // 2))

        @pl.when(r >= n_a + n_b)
        def _():
            j = r - n_a - n_b
            load_tile(k, 0, 0, down_tile(l, n_b + 2 * j))
            load_tile(k, 1, 1, out_tile(l, j))
            load_tile(k, 2, 2, down_tile(l, n_b + 2 * j + 1))

        @pl.when((r >= n_a + 4) & (r < n_a + n_b + 4))
        def _():
            load_tile(k, 1, 3, down_tile(l, r - n_a - 4))

    def loaded(slot, to):
        pltpu.make_async_copy(wbuf.at[slot, to], wbuf.at[slot, to], ld.at[slot, to]).wait()

    def within(k, do):
        @pl.when((k >= 0) & (k < chunks))
        def _():
            do(k)

    def sub0(t):
        within(t - 8, wait_sent)
        within(t, send_own)
        within(t - 4, lambda k: pass_on(k, 3))
        within(t - 4, lambda k: pass_mate(k, 2))

    def sub1(t):
        within(t - 1, lambda k: pass_on(k, 1))
        within(t - 5, lambda k: pass_mate(k, 3))

    def sub2(t):
        within(t - 2, lambda k: pass_on(k, 2))
        within(t - 2, lambda k: pass_mate(k, 1))
        within(t - 5, wait_sib)
        within(t - 5, load)

    blocks = seq // ROWS

    def rows_of(b):
        return pl.ds(b * ROWS, ROWS)

    def cols_of(j):
        return pl.ds(pl.multiple_of(j * tile, tile), tile)

    def row(s, l, i):
        return smallg[s, l, pl.ds(i, 1), :]

    def layer_norms(l):
        step = 128

        def body(b, carry):
            rows = pl.ds(pl.multiple_of(b * step, step), step)
            v = xs[rows, :].astype(F32)
            cen = v - jnp.mean(v, axis=-1, keepdims=True)
            inv = lax.rsqrt(jnp.mean(cen * cen, axis=-1, keepdims=True) + LN_EPS)
            for s in range(n):
                cols = pl.ds(s * tile, tile)
                norm = cen[:, s * tile:(s + 1) * tile] * inv
                a_s[rows, cols] = (norm * row(s, l, 0) + row(s, l, 1)).astype(BF16)
                m_s[rows, cols] = (norm * row(s, l, 2) + row(s, l, 3)).astype(BF16)
                acc[rows, cols] = v[:, s * tile:(s + 1) * tile] + (row(s, l, 7) + row(s, l, 8 + rps))
            return carry

        lax.fori_loop(0, seq // step, body, 0)

    def dot(lhs, slot, to):
        return jnp.dot(lhs, wbuf[slot, to], preferred_element_type=F32)

    def rotate(v, rows):
        u = v[:, :wide].astype(F32)
        turned = (u * tabs[0, rows, :] + pltpu.roll(u, wide - rot_half, 1) * tabs[1, rows, :]
                  + pltpu.roll(u, rot_half, 1) * tabs[2, rows, :])
        return turned.astype(BF16)

    def project(l, h, slot, i, ref):
        for b in range(blocks):
            v = (dot(a_s[rows_of(b), :], slot, i) + row(h, l, 4 + i)).astype(BF16)
            if i < 2:
                ref[rows_of(b), pl.ds(0, wide)] = rotate(v, rows_of(b))
                ref[rows_of(b), pl.ds(wide, tile - wide)] = v[:, wide:]
            else:
                ref[rows_of(b), :] = v

    def attend(h, b):
        width = (b + 1) * ROWS
        s = lax.dot_general(q_s[rows_of(b), :], k_s[pl.ds(0, width), :], (((1,), (1,)), ((), ())),
                            preferred_element_type=F32) * scale
        col = lax.broadcasted_iota(jnp.int32, (ROWS, width), 1)
        at = lax.broadcasted_iota(jnp.int32, (ROWS, width), 0) + b * ROWS
        s = jnp.where((col <= at) & (col < lens[0:1, 0:1]), s, -1e30)
        e = jnp.exp(s - jnp.max(s, axis=-1, keepdims=True))
        p = (e * (1.0 / jnp.sum(e, axis=-1, keepdims=True))).astype(BF16)
        ctx[rows_of(b), cols_of(h)] = jnp.dot(p, v_s[pl.ds(0, width), :], preferred_element_type=F32).astype(BF16)

    def up(l, u, slot, to):
        s, rp = u % n, u // n
        for b in range(blocks):
            v = dot(m_s[rows_of(b), :], slot, to) + row(s, l, 8 + rp)
            g = (0.5 * v) * (1.0 + lax.erf(v * (0.5 ** 0.5)))
            act[rp, rows_of(b), cols_of(s)] = g.astype(BF16)

    def add_to(j, slot, to, lhs):
        for b in range(blocks):
            acc[rows_of(b), cols_of(j)] += dot(lhs(rows_of(b)), slot, to)

    def down(v, slot, to):
        add_to(v % n_c, slot, to, lambda rows: act[v // n_c, rows, :])

    def head_step(l, h):
        k = l * per_layer + h
        t, slot = k + LAG, k % 2
        sub0(t)
        for i in range(3):
            loaded(slot, i)
        project(l, h, slot, 0, q_s)
        project(l, h, slot, 1, k_s)
        sub1(t)
        project(l, h, slot, 2, v_s)
        for b in range(blocks // 2):
            attend(h, b)
        sub2(t)
        for b in range(blocks // 2, blocks):
            attend(h, b)

    def up_step(l, j):
        k = l * per_layer + n_a + j
        t, slot = k + LAG, k % 2
        sub0(t)
        loaded(slot, 0)
        up(l, 2 * j, slot, 0)
        sub1(t)
        loaded(slot, 2)
        up(l, 2 * j + 1, slot, 2)
        sub2(t)

        @pl.when(j >= 4)
        def _():
            loaded(slot, 3)
            down(j - 4, slot, 3)

    def down_step(l, j):
        k = l * per_layer + n_a + n_b + j
        t, slot = k + LAG, k % 2
        sub0(t)
        loaded(slot, 0)
        down(n_b + 2 * j, slot, 0)
        sub1(t)
        loaded(slot, 2)
        down(n_b + 2 * j + 1, slot, 2)
        sub2(t)
        loaded(slot, 1)
        add_to(j, slot, 1, lambda rows: ctx[rows, :])

        @pl.when(j < 4)
        def _():
            loaded(slot, 3)
            down(n_b - 4 + j, slot, 3)

    get_hidden = pltpu.make_async_copy(hid, xs, io_sem)
    get_hidden.start()
    barrier = pltpu.get_barrier_semaphore()
    for step in range(1, n):
        pl.semaphore_signal(barrier, inc=1, device_id={"fsdp": (f + step) % n}, device_id_type=MESH)
    pl.semaphore_signal(barrier, inc=1, device_id=to_mate, device_id_type=MESH)
    pl.semaphore_wait(barrier, n)

    sub0(0)
    smalls = [
        remote(small, smallg.at[f], small_send.at[step - 1], small_recv.at[step - 1], {"fsdp": (f + step) % n})
        for step in range(1, n)
    ]
    for copy in smalls:
        copy.start()
    smallg[f] = small[...]
    sub0(1)
    sub1(1)
    for copy in smalls:
        copy.wait()
    get_hidden.wait()
    layer_norms(0)
    sub2(1)

    def fill(t, carry):
        sub0(t)
        sub1(t)
        sub2(t)
        return carry

    lax.fori_loop(2, LAG, fill, 0)

    def layer(l, carry):
        def loop(count, step):
            def body(i, inner):
                step(l, i)
                return inner

            lax.fori_loop(0, count, body, 0)

        @pl.when(l > 0)
        def _():
            layer_norms(l)

        loop(n_a, head_step)
        loop(n_b, up_step)
        loop(n_c, down_step)
        for b in range(blocks):
            xs[rows_of(b), :] = acc[rows_of(b), :].astype(BF16)
        return carry

    lax.fori_loop(0, num_layers, layer, 0)
    put = pltpu.make_async_copy(xs, out, io_sem)
    put.start()
    wait_sent(chunks - 2)
    wait_sent(chunks - 1)
    put.wait()


def solution(mesh):
    row_spec = P(("dp", "fsdp"), None, None)
    in_specs = (row_spec, P(("dp", "fsdp")), P(None, None, "fsdp"), P(None, "fsdp", None, None), P(None, "fsdp"),
                P(None, "fsdp", None), P(None, "fsdp"), P(None, "fsdp", None), P(None, "fsdp"), P(None, "fsdp", None),
                P(None, "fsdp"))
    n = mesh.shape["fsdp"]
    assert n % 2 == 0 and mesh.shape["dp"] % 2 == 0

    def local_step(hidden, lens, ln_par, w_qkv, b_qkv, w_out, b_out, w_up, b_up, w_down, b_down):
        _, seq, d_model = hidden.shape
        num_layers, tile, heads, triple = w_qkv.shape
        rps = w_down.shape[1] // tile
        assert hidden.shape[0] == 1 and n * tile == d_model and triple == 3 * tile and heads == n
        assert n * rps // 2 + 2 * (d_model // tile) == n * rps
        rot_half = tile // 8
        wide = 128
        per = [(num_layers, -1, tile)] * 4
        small = jnp.concatenate(
            [ln_par] + [b.astype(F32).reshape(p) for b, p in zip((b_qkv, b_out, b_up, b_down), per)], axis=1)
        small = jnp.pad(small, ((0, 0), (0, -small.shape[1] % 8), (0, 0)))
        tabs = rope_tables(seq, 2 * rot_half, wide)
        dims = (n, num_layers, heads, tile, seq, d_model, rps, rot_half)
        chunks = num_layers * (heads + n * rps // 2 + d_model // tile)
        ring = n // 2
        vmem = pl.BlockSpec(memory_space=pltpu.VMEM)
        anywhere = pl.BlockSpec(memory_space=pl.ANY)
        dma = pltpu.SemaphoreType.DMA
        out, _ = pl.pallas_call(
            functools.partial(kernel, dims),
            name="layers",
            out_shape=(jax.ShapeDtypeStruct((seq, d_model), BF16),
                       jax.ShapeDtypeStruct((chunks, 3, n, tile, tile), BF16)),
            in_specs=[anywhere, vmem, vmem, vmem] + [anywhere] * 4,
            out_specs=(anywhere, anywhere),
            scratch_shapes=[
                pltpu.VMEM((seq, d_model), BF16),
                pltpu.VMEM((seq, d_model), BF16),
                pltpu.VMEM((seq, d_model), BF16),
                pltpu.VMEM((seq, d_model), BF16),
                pltpu.VMEM((rps, seq, d_model), BF16),
                pltpu.VMEM((seq, d_model), F32),
                pltpu.VMEM((seq, tile), BF16),
                pltpu.VMEM((seq, tile), BF16),
                pltpu.VMEM((seq, tile), BF16),
                pltpu.VMEM((2, 4, d_model, tile), BF16),
                pltpu.VMEM((n,) + small.shape, F32),
                dma((SLOTS,)),
                dma((SLOTS, ring - 1)),
                dma((SLOTS, ring - 1)),
                dma((SLOTS, ring - 1)),
                dma((SLOTS,)),
                dma((2, 4)),
                dma((n - 1,)),
                dma((n - 1,)),
                dma,
            ],
            compiler_params=pltpu.CompilerParams(
                collective_id=0, has_side_effects=True, vmem_limit_bytes=67043328),
        )(hidden.reshape(seq, d_model), jnp.broadcast_to(lens.reshape(1, 1), (8, 128)), small, tabs,
          w_qkv.reshape(num_layers, tile, heads * triple), w_out, w_up, w_down)
        return out.reshape(1, seq, d_model)

    return jax.shard_map(local_step, mesh=mesh, in_specs=in_specs, out_specs=row_spec, check_vma=False)
```

time: 1010 us -> 598 us (0.59)
  Pallas kernels: 0 us -> 573 us
  matrix products: 490 us -> 0 us
  blocking collectives: 220 us -> 0 us
  local copies, waits for them, and re-layouts: 143 us -> 19.8 us
  other arithmetic: 117 us -> 3.69 us
  waiting for transfers between devices: 16.9 us -> 0 us
  between operations: 14.9 us -> 0.69 us
    pallas_call x0 -> x1, Pallas kernels: none -> 573 us  [local_step(): pl.pallas_call(functools.partial(kernel, dims), name='layers', out_shape=...]
    dot_general x12 -> x0, matrix products: 490 us -> none  [the longest x2 238 us: layer_forward(): jnp.dot(mlp_in, w_up_full, preferred_element_type=jnp.float32)]
    all_gather x10 -> x0, blocking collectives: 220 us -> none  [gather_full(): return lax.all_gather(piece, 'fsdp', axis=axis_idx, tiled=True)]
    unnamed x89 -> x1, local copies, waits for them, and re-layouts: 90.5 us -> 4.79 us
    sub x2 -> x0, other arithmetic: 67.2 us -> none  [attention_core(): jax.nn.softmax(jnp.where(visible, scores, -1e+30), axis=-1)]
    slice x17 -> x0, local copies, waits for them, and re-layouts: 36 us -> none  [the longest x2 11.1 us: apply_rotary(): head_vals[..., rot_dim:]]
    convert_element_type x13 -> x0, other arithmetic: 23.4 us -> none  [the longest x2 13.9 us: apply_rotary(): rotated.astype(jnp.bfloat16)]
    convert_element_type x1 -> x0, local copies, waits for them, and re-layouts: 16.6 us -> none  [layer_forward(): qkv_rows.astype(jnp.bfloat16)]
  transfers between devices with their start and end apart: 8 -> 0, of which waited for: 1 -> 0; matrix products, arithmetic and copies ran while one was open for 72% -> 0% of each run, Pallas kernels for 0% -> 0%
where the time goes in v1:
time: 598 us; the launch traced here: 597 us
  Pallas kernels  573 us (96%)
  local copies, waits for them, and re-layouts  19.8 us (3%)
    pallas_call x1, Pallas kernels, local_step(): pl.pallas_call(functools.partial(kernel, dims), name='layers', out_shape=...  573 us

profile of v1, /device:TPU:113, one launch (start us, length us, event | category | flops | bytes accessed | tf_op | source)
XLA Modules:
  0.0 597.3 jit_solution(5373392345508026758)
XLA Ops:
  0.7 0.1 pad.13.clone
  0.7 0.1 pad.16.clone
  0.8 0.7 reshape.55
  1.5 0.7 reshape.59
  2.2 0.6 broadcast_in_dim.19.lens
  2.8 0.7 reshape.53
  3.5 0.7 reshape.57
  4.2 0.7 concatenate.12
  4.9 0.6 pad.4.small
  5.6 2.0 fusion.1
  7.6 0.5 maximum_bitcast_fusion.1
  8.0 1.2 pad_maximum_fusion.tabs
  9.3 10.1 %reshape.50.wq = bf16[2,256,6144]{2,1,0:T(8,128)(2,1)} reshape(bf16[2,256,8,768]{3,2,1,0:T(8,128)(2,1)} %param.14) | data formatting | bytes 12582912 | tf_op jit(solution)/shard_map/reshape | solution.py:435
  19.4 573.1 %layers.1 = (bf16[1024,2048]{1,0:T(8,128)(2,1)}, bf16[64,3,8,256,256]{4,3,2,1,0:T(8,128)(2,1)}) custom-call(bf16[1024,2048]{1,0:T(8,128)(2,1)} %bitcast.12, s32[8,128]{1,0:T(8,128)} %broadcast_in_dim.19.lens, f32[2,16,256]{2,1,0:T(8,128)} %pad.4.small, f32[3,1024,128]{2,1,0:T(8,128)} %pad_maximum_fusion.tabs, bf16[2,256,6144]{2,1,0:T(8,128)(2,1)} %reshape.50.wq, ...), custom_call_target="tpu_custom_call" | custom-call | tf_op jit(solution)/shard_map/layers/pallas_call | solution.py:403
  592.5 4.8 copy.14
  (4 shorter events, 0.1 us)

commit v2 on v1

v2 whole, which is shorter than its diff:
```python
import functools

import jax
import jax.numpy as jnp
import numpy as np
from jax import lax
from jax.experimental import pallas as pl
from jax.experimental.pallas import tpu as pltpu
from jax.sharding import PartitionSpec as P

ROPE_BASE = 10000.0
LN_EPS = 1e-5
MESH = pl.DeviceIdType.MESH
SLOTS = 16
LATE = 4
ROWS = 256
F32 = jnp.float32
BF16 = jnp.bfloat16


def rope_row(rot_dim, width):
    inv_freq = np.float32(1.0) / (np.float32(ROPE_BASE) ** (np.arange(0, rot_dim, 2, dtype=np.float32) / np.float32(rot_dim)))
    row = np.concatenate([inv_freq, inv_freq, np.zeros(width - rot_dim, np.float32)])
    return np.broadcast_to(row.astype(np.float32), (8, width))


def kernel(dims, hid, lens, freq, ln_own, bq_own, bo_own, bu_own, bd_own, wq_raw, wo, wu, wd, out, gath, wq, xs, a_s, m_s, ctx,
           act, acc, q_s, k_s, v_s, wbuf, tabs, ln_g, bq_g, bo_g, bu_g, bd_g, bias, raw, raw32, turned, send, rs, ls, ysem, dd,
           ld, small_send, small_recv, raw_in, raw_out, io_sem):
    n, num_layers, heads, tile, seq, d_model, rps, rot_half = dims
    ring = n // 2
    n_a, n_b, n_c = heads, n * rps // 2, d_model // tile
    per_layer = n_a + n_b + n_c
    chunks = num_layers * per_layer
    wide = tabs.shape[2]
    scale = float(tile) ** -0.5

    d, f = lax.axis_index("dp"), lax.axis_index("fsdp")
    x, c = f // 2, f % 2
    par = d % 2
    right = ((x + 1) % ring) * 2 + c
    left = ((x + ring - 1) % ring) * 2 + c
    far = ((x + 2) % ring) * 2 + c
    sib = x * 2 + 1 - c
    mate = d + 1 - 2 * par
    mine, other = 2 * par, 2 - 2 * par

    def remote(src, dst, s_sem, r_sem, where):
        return pltpu.make_async_remote_copy(
            src_ref=src, dst_ref=dst, send_sem=s_sem, recv_sem=r_sem, device_id=where, device_id_type=MESH)

    to_right, to_left, to_sib, to_mate = {"fsdp": right}, {"fsdp": left}, {"fsdp": sib}, {"dp": mate}

    def q_tile(l, h, i):
        return wq.at[l, h, :, pl.ds(i * tile, tile) if isinstance(i, int) else pl.ds(pl.multiple_of(i * tile, tile), tile)]

    def up_tile(l, u):
        return wu.at[l, :, pl.ds(pl.multiple_of((u % n) * (rps * tile) + (u // n) * tile, tile), tile)]

    def down_tile(l, v):
        return wd.at[l, pl.ds(pl.multiple_of((v // n_c) * tile, tile), tile),
                     pl.ds(pl.multiple_of((v % n_c) * tile, tile), tile)]

    def out_tile(l, j):
        return wo.at[l, :, pl.ds(pl.multiple_of(j * tile, tile), tile)]

    def with_own(k, go):
        l, r = k // per_layer, k % per_layer

        @pl.when(r < n_b)
        def _():
            go(lambda i: down_tile(l, r) if isinstance(i, int) and i == 1 else up_tile(l, 2 * r + i // 2))

        @pl.when((r >= n_b) & (r < n_b + n_a))
        def _():
            go(lambda i: q_tile(l, r - n_b, i))

        @pl.when(r >= n_a + n_b)
        def _():
            j = r - n_a - n_b
            go(lambda i: out_tile(l, j) if isinstance(i, int) and i == 1 else down_tile(l, n_b + 2 * j + i // 2))

    def own_first(k):
        slot = k % SLOTS

        def go(own):
            remote(own(mine), gath.at[k, mine, f], send.at[slot], rs.at[slot, 0], to_right).start()
            remote(own(1), gath.at[k, 1, f], send.at[slot], ls.at[slot, 0], to_left).start()
            for i in (mine, 1):
                remote(own(i), gath.at[k, i, f], send.at[slot], dd.at[slot], to_sib).start()

        with_own(k, go)

    def own_second(k):
        slot = k % SLOTS

        def go(own):
            remote(own(1), gath.at[k, 1, f], send.at[slot], rs.at[slot, 1], to_right).start()
            remote(own(mine), gath.at[k, mine, f], send.at[slot], ls.at[slot, 1], to_left).start()
            remote(own(other), gath.at[k, other, f], send.at[slot], dd.at[slot], to_sib).start()

        with_own(k, go)

    def wait_tile(sem):
        ref = gath.at[0, 0, 0]
        pltpu.make_async_copy(ref, ref, sem).wait()

    def pass_on(k, i, s, sem, where):
        t = gath.at[k, i, s]
        remote(t, t, send.at[k % SLOTS], sem, where).start()

    def from_sides(k):
        slot = k % SLOTS
        wait_tile(rs.at[slot, 0])
        pass_on(k, mine, left, rs.at[slot, 2], to_right)
        pass_on(k, mine, left, ysem.at[slot, 0], to_mate)
        pass_on(k, mine, left, dd.at[slot], to_sib)
        wait_tile(ls.at[slot, 0])
        pass_on(k, 1, right, ls.at[slot, 2], to_left)
        pass_on(k, 1, right, dd.at[slot], to_sib)

    def from_sides_again(k):
        slot = k % SLOTS
        wait_tile(ls.at[slot, 1])
        pass_on(k, mine, right, ysem.at[slot, 1], to_mate)
        pass_on(k, mine, right, dd.at[slot], to_sib)
        wait_tile(rs.at[slot, 1])
        pass_on(k, 1, left, dd.at[slot], to_sib)

    def from_far(k):
        slot = k % SLOTS
        wait_tile(rs.at[slot, 2])
        pass_on(k, mine, far, ysem.at[slot, 2], to_mate)
        pass_on(k, mine, far, dd.at[slot], to_sib)
        wait_tile(ls.at[slot, 2])
        pass_on(k, 1, far, dd.at[slot], to_sib)

    def from_mate(i, s):
        def do(k):
            slot = k % SLOTS
            wait_tile(ysem.at[slot, i])
            pass_on(k, other, s, dd.at[slot], to_sib)

        return do

    sib_tiles = 3 * ring
    sent_tiles = 3 * (ring - 1) + sib_tiles

    def wait_sib(k):
        ref = gath.at[0, :, pl.ds(0, sib_tiles // 3)]
        pltpu.make_async_copy(ref, ref, dd.at[k % SLOTS]).wait()

    def wait_sent(k):
        ref = gath.at[0, :, pl.ds(0, sent_tiles // 3)]
        pltpu.make_async_copy(ref, ref, send.at[k % SLOTS]).wait()

    def load_tile(k, kk, i, to, own):
        slot = k % 2
        for step in range(1, n):
            s = (f + step) % n
            pltpu.make_async_copy(
                gath.at[kk, i, s], wbuf.at[slot, to, pl.ds(pl.multiple_of(s * tile, tile), tile)], ld.at[slot, to]).start()
        pltpu.make_async_copy(own, wbuf.at[slot, to, pl.ds(pl.multiple_of(f * tile, tile), tile)], ld.at[slot, to]).start()

    def load(k):
        l, r = k // per_layer, k % per_layer
        j = r - n_a - n_b

        @pl.when(r < n_b)
        def _():
            for i in (0, 2):
                load_tile(k, k, i, i, up_tile(l, 2 * r + i // 2))

        @pl.when((r >= LATE) & (r < n_b))
        def _():
            load_tile(k, k - LATE, 1, 3, down_tile(l, r - LATE))

        @pl.when((r >= n_b) & (r < n_b + n_a))
        def _():
            for i in range(3):
                load_tile(k, k, i, i, q_tile(l, r - n_b, i))

        @pl.when(r >= n_a + n_b)
        def _():
            load_tile(k, k, 0, 0, down_tile(l, n_b + 2 * j))
            load_tile(k, k, 1, 1, out_tile(l, j))
            load_tile(k, k, 2, 2, down_tile(l, n_b + 2 * j + 1))

        @pl.when((r >= n_a + n_b) & (j < LATE))
        def _():
            load_tile(k, k - n_a - LATE, 1, 3, down_tile(l, n_b - LATE + j))

    def loaded(slot, to):
        pltpu.make_async_copy(wbuf.at[slot, to], wbuf.at[slot, to], ld.at[slot, to]).wait()

    def within(k, do):
        @pl.when((k >= 0) & (k < chunks))
        def _():
            do(k)

    def part0(t):
        within(t - 7, wait_sent)
        within(t, own_first)
        within(t - 2, from_sides_again)
        within(t - 4, wait_sib)
        within(t - 4, load)

    def part1(t):
        within(t - 1, from_sides)
        within(t - 3, from_mate(1, right))

    def part2(t):
        within(t, own_second)
        within(t - 2, from_far)
        within(t - 2, from_mate(0, left))
        within(t - 3, from_mate(2, far))

    blocks = seq // ROWS

    def rows_of(b):
        return pl.ds(b * ROWS, ROWS)

    def cols_of(j):
        return pl.ds(pl.multiple_of(j * tile, tile), tile)

    def row(s, l, i):
        return bias[s, l, pl.ds(i, 1), :]

    def ln_row(s, l, i):
        return ln_g[s, l, pl.ds(i, 1), :]

    def layer_norms(l):
        step = 128

        def body(b, carry):
            rows = pl.ds(pl.multiple_of(b * step, step), step)
            v = xs[rows, :].astype(F32)
            cen = v - jnp.mean(v, axis=-1, keepdims=True)
            inv = lax.rsqrt(jnp.mean(cen * cen, axis=-1, keepdims=True) + LN_EPS)
            for s in range(n):
                cols = pl.ds(s * tile, tile)
                norm = cen[:, s * tile:(s + 1) * tile] * inv
                a_s[rows, cols] = (norm * ln_row(s, l, 0) + ln_row(s, l, 1)).astype(BF16)
                m_s[rows, cols] = (norm * ln_row(s, l, 2) + ln_row(s, l, 3)).astype(BF16)
                acc[rows, cols] = v[:, s * tile:(s + 1) * tile] + (row(s, l, 3) + row(s, l, 4 + rps))
            return carry

        lax.fori_loop(0, seq // step, body, 0)

    def dot(lhs, slot, to):
        return jnp.dot(lhs, wbuf[slot, to], preferred_element_type=F32)

    def rotate(v, rows):
        u = v[:, :wide].astype(F32)
        turned = (u * tabs[0, rows, :] + pltpu.roll(u, wide - rot_half, 1) * tabs[1, rows, :]
                  + pltpu.roll(u, rot_half, 1) * tabs[2, rows, :])
        return turned.astype(BF16)

    def project(l, h, slot, i, ref):
        for b in range(blocks):
            v = (dot(a_s[rows_of(b), :], slot, i) + row(h, l, i)).astype(BF16)
            if i < 2:
                ref[rows_of(b), pl.ds(0, wide)] = rotate(v, rows_of(b))
                ref[rows_of(b), pl.ds(wide, tile - wide)] = v[:, wide:]
            else:
                ref[rows_of(b), :] = v

    def attend(h, b):
        width = (b + 1) * ROWS
        s = lax.dot_general(q_s[rows_of(b), :], k_s[pl.ds(0, width), :], (((1,), (1,)), ((), ())),
                            preferred_element_type=F32) * scale
        col = lax.broadcasted_iota(jnp.int32, (ROWS, width), 1)
        at = lax.broadcasted_iota(jnp.int32, (ROWS, width), 0) + b * ROWS
        s = jnp.where((col <= at) & (col < lens[0]), s, -1e30)
        e = jnp.exp(s - jnp.max(s, axis=-1, keepdims=True))
        p = (e * (1.0 / jnp.sum(e, axis=-1, keepdims=True))).astype(BF16)
        ctx[rows_of(b), cols_of(h)] = jnp.dot(p, v_s[pl.ds(0, width), :], preferred_element_type=F32).astype(BF16)

    def up(l, u, slot, to):
        s, rp = u % n, u // n
        for b in range(blocks):
            v = dot(m_s[rows_of(b), :], slot, to) + row(s, l, 4 + rp)
            g = (0.5 * v) * (1.0 + lax.erf(v * (0.5 ** 0.5)))
            act[rp, rows_of(b), cols_of(s)] = g.astype(BF16)

    def add_to(j, slot, to, lhs):
        for b in range(blocks):
            acc[rows_of(b), cols_of(j)] += dot(lhs(rows_of(b)), slot, to)

    def down(v, slot, to):
        add_to(v % n_c, slot, to, lambda rows: act[v // n_c, rows, :])

    def head_step(l, h):
        k = l * per_layer + n_b + h
        slot = k % 2
        part1(k + 4)
        loaded(slot, 0)
        loaded(slot, 1)
        project(l, h, slot, 0, q_s)
        project(l, h, slot, 1, k_s)
        part2(k + 4)
        loaded(slot, 2)
        project(l, h, slot, 2, v_s)
        for b in range(blocks // 2):
            attend(h, b)
        part0(k + 5)
        for b in range(blocks // 2, blocks):
            attend(h, b)

    def up_step(l, j):
        k = l * per_layer + j
        slot = k % 2
        part1(k + 4)
        loaded(slot, 0)
        up(l, 2 * j, slot, 0)
        part2(k + 4)
        loaded(slot, 2)
        up(l, 2 * j + 1, slot, 2)
        part0(k + 5)

        @pl.when(j >= LATE)
        def _():
            loaded(slot, 3)
            down(j - LATE, slot, 3)

    def down_step(l, j):
        k = l * per_layer + n_a + n_b + j
        slot = k % 2
        part1(k + 4)
        loaded(slot, 0)
        down(n_b + 2 * j, slot, 0)

        @pl.when(j < LATE)
        def _():
            loaded(slot, 3)
            down(n_b - LATE + j, slot, 3)

        part2(k + 4)
        loaded(slot, 2)
        down(n_b + 2 * j + 1, slot, 2)
        part0(k + 5)
        loaded(slot, 1)
        add_to(j, slot, 1, lambda rows: ctx[rows, :])

    def rotary_tables():
        for b in range(blocks):
            at = (lax.broadcasted_iota(jnp.int32, (ROWS, wide), 0) + b * ROWS).astype(F32)
            lane = lax.broadcasted_iota(jnp.int32, (ROWS, wide), 1)
            angle = at * freq[0:1, :]
            cos, sin = jnp.cos(angle), jnp.sin(angle)
            tabs[0, rows_of(b), :] = jnp.where(lane < 2 * rot_half, cos, 1.0)
            tabs[1, rows_of(b), :] = jnp.where(lane < rot_half, -sin, 0.0)
            tabs[2, rows_of(b), :] = jnp.where((lane >= rot_half) & (lane < 2 * rot_half), sin, 0.0)

    raw_rows = raw.shape[1]
    per_raw = tile * heads // raw_rows
    raws = num_layers * per_raw

    def get_raw(b):
        return pltpu.make_async_copy(
            wq_raw.at[b // per_raw, pl.ds(pl.multiple_of((b % per_raw) * raw_rows, raw_rows), raw_rows)],
            raw.at[b % 2], raw_in.at[b % 2])

    def put_raw(b):
        some = raw_rows // heads
        return pltpu.make_async_copy(
            turned.at[b % 2], wq.at[b // per_raw, :, pl.ds(pl.multiple_of((b % per_raw) * some, some), some)],
            raw_out.at[b % 2])

    def by_head(first, last):
        def body(b, carry):
            get_raw(b).wait()
            for q in range(raw.shape[2] // wide):
                raw32[pl.ds(q * raw_rows, raw_rows), :] = raw[b % 2, :, pl.ds(q * wide, wide)].astype(F32)

            @pl.when(b + 2 < raws)
            def _():
                get_raw(b + 2).start()

            @pl.when(b >= 2)
            def _():
                put_raw(b - 2).wait()

            for h in range(heads):
                for q in range(raw.shape[2] // wide):
                    turned[b % 2, h, :, pl.ds(q * wide, wide)] = (
                        raw32[pl.ds(q * raw_rows + h, raw_rows // heads, stride=heads), :].astype(BF16))
            put_raw(b).start()
            return carry

        lax.fori_loop(first, last, body, 0)

    def unpack_biases():
        for s in range(n):
            for g, at, count in ((bq_g, 0, 3), (bo_g, 3, 1), (bu_g, 4, rps), (bd_g, 4 + rps, 1)):
                for i in range(count):
                    v = g[s, :, pl.ds(i * tile, tile)].astype(F32)
                    for l in range(num_layers):
                        bias[s, l, pl.ds(at + i, 1), :] = v[l:l + 1]

    get_hidden = pltpu.make_async_copy(hid, xs, io_sem)
    get_hidden.start()
    get_raw(0).start()
    get_raw(1).start()
    barrier = pltpu.get_barrier_semaphore()
    for step in range(1, n):
        pl.semaphore_signal(barrier, inc=1, device_id={"fsdp": (f + step) % n}, device_id_type=MESH)
    pl.semaphore_signal(barrier, inc=1, device_id=to_mate, device_id_type=MESH)
    pl.semaphore_wait(barrier, n)

    own_first(0)
    own_second(0)
    part0(1)
    smalls = ((ln_own, ln_g), (bq_own, bq_g), (bo_own, bo_g), (bu_own, bu_g), (bd_own, bd_g))
    for i, (own, everyone) in enumerate(smalls):
        for step in range(1, n):
            remote(own, everyone.at[f], small_send.at[i], small_recv.at[i], {"fsdp": (f + step) % n}).start()
        everyone[f] = own[...]
    rotary_tables()
    part1(1)
    for i, (own, everyone) in enumerate(smalls):
        ref = everyone.at[pl.ds(0, n - 1)]
        pltpu.make_async_copy(ref, ref, small_send.at[i]).wait()
        pltpu.make_async_copy(ref, ref, small_recv.at[i]).wait()
    unpack_biases()
    part2(1)
    get_hidden.wait()
    layer_norms(0)
    cuts = [raws * i // 6 for i in range(7)]
    for i, (part, t) in enumerate(((part0, 2), (part1, 2), (part2, 2), (part0, 3), (part1, 3), (part2, 3))):
        part(t)
        by_head(cuts[i], cuts[i + 1])
    put_raw(raws - 2).wait()
    put_raw(raws - 1).wait()
    part0(4)

    def layer(l, carry):
        def loop(count, step):
            def body(i, inner):
                step(l, i)
                return inner

            lax.fori_loop(0, count, body, 0)

        @pl.when(l > 0)
        def _():
            layer_norms(l)

        loop(n_b, up_step)
        loop(n_a, head_step)
        loop(n_c, down_step)
        for b in range(blocks):
            xs[rows_of(b), :] = acc[rows_of(b), :].astype(BF16)
        return carry

    lax.fori_loop(0, num_layers, layer, 0)
    put = pltpu.make_async_copy(xs, out, io_sem)
    put.start()
    wait_sent(chunks - 2)
    wait_sent(chunks - 1)
    put.wait()


def solution(mesh):
    row_spec = P(("dp", "fsdp"), None, None)
    in_specs = (row_spec, P(("dp", "fsdp")), P(None, None, "fsdp"), P(None, "fsdp", None, None), P(None, "fsdp"),
                P(None, "fsdp", None), P(None, "fsdp"), P(None, "fsdp", None), P(None, "fsdp"), P(None, "fsdp", None),
                P(None, "fsdp"))
    n = mesh.shape["fsdp"]
    assert n % 2 == 0 and mesh.shape["dp"] % 2 == 0

    def local_step(hidden, lens, ln_par, w_qkv, b_qkv, w_out, b_out, w_up, b_up, w_down, b_down):
        _, seq, d_model = hidden.shape
        num_layers, tile, heads, triple = w_qkv.shape
        rps = w_down.shape[1] // tile
        assert hidden.shape[0] == 1 and n == 8 and n * tile == d_model and triple == 3 * tile and heads == n
        assert n * rps // 2 + 2 * (d_model // tile) == n * rps
        rot_half = tile // 8
        wide = 128
        raw_rows = 32 * heads
        dims = (n, num_layers, heads, tile, seq, d_model, rps, rot_half)
        chunks = num_layers * (heads + n * rps // 2 + d_model // tile)
        ring = n // 2
        vmem = pl.BlockSpec(memory_space=pltpu.VMEM)
        anywhere = pl.BlockSpec(memory_space=pl.ANY)
        dma = pltpu.SemaphoreType.DMA
        smalls = (ln_par, b_qkv, b_out, b_up, b_down)
        out, _, _ = pl.pallas_call(
            functools.partial(kernel, dims),
            name="layers",
            out_shape=(jax.ShapeDtypeStruct((seq, d_model), BF16),
                       jax.ShapeDtypeStruct((chunks, 3, n, tile, tile), BF16),
                       jax.ShapeDtypeStruct((num_layers, heads, tile, triple), BF16)),
            in_specs=[anywhere, pl.BlockSpec(memory_space=pltpu.SMEM), vmem] + [vmem] * 5 + [anywhere] * 4,
            out_specs=(anywhere, anywhere, anywhere),
            scratch_shapes=[
                pltpu.VMEM((seq, d_model), BF16),
                pltpu.VMEM((seq, d_model), BF16),
                pltpu.VMEM((seq, d_model), BF16),
                pltpu.VMEM((seq, d_model), BF16),
                pltpu.VMEM((rps, seq, d_model), BF16),
                pltpu.VMEM((seq, d_model), F32),
                pltpu.VMEM((seq, tile), BF16),
                pltpu.VMEM((seq, tile), BF16),
                pltpu.VMEM((seq, tile), BF16),
                pltpu.VMEM((2, 4, d_model, tile), BF16),
                pltpu.VMEM((3, seq, wide), F32),
                *[pltpu.VMEM((n,) + p.shape, p.dtype) for p in smalls],
                pltpu.VMEM((n, num_layers, 16, tile), F32),
                pltpu.VMEM((2, raw_rows, triple), BF16),
                pltpu.VMEM((raw_rows * triple // wide, wide), F32),
                pltpu.VMEM((2, heads, raw_rows // heads, triple), BF16),
                dma((SLOTS,)),
                dma((SLOTS, 3)),
                dma((SLOTS, 3)),
                dma((SLOTS, 3)),
                dma((SLOTS,)),
                dma((2, 4)),
                dma((5,)),
                dma((5,)),
                dma((2,)),
                dma((2,)),
                dma,
            ],
            compiler_params=pltpu.CompilerParams(
                collective_id=0, has_side_effects=True, vmem_limit_bytes=67043328),
        )(hidden.reshape(seq, d_model), lens, jnp.asarray(rope_row(2 * rot_half, wide)), *smalls,
          w_qkv.reshape(num_layers, tile * heads, triple), w_out, w_up, w_down)
        return out.reshape(1, seq, d_model)

    return jax.shard_map(local_step, mesh=mesh, in_specs=in_specs, out_specs=row_spec, check_vma=False)
```

time: 598 us -> 580 us (0.970)
  local copies, waits for them, and re-layouts: 19.8 us -> 6.04 us
    reshape x5 -> x0, local copies, waits for them, and re-layouts: 12.9 us -> none  [the longest x1 10.1 us: local_step(): w_qkv.reshape(num_layers, tile, heads * triple)]
where the time goes in v2:
time: 580 us; the launch traced here: 579 us
  Pallas kernels  572 us (99%)
  local copies, waits for them, and re-layouts  6.04 us (1%)
    pallas_call x1, Pallas kernels, local_step(): pl.pallas_call(functools.partial(kernel, dims), name='layers', out_shape=...  572 us

profile of v2, /device:TPU:113, one launch (start us, length us, event | category | flops | bytes accessed | tf_op | source)
XLA Modules:
  0.0 578.9 jit_solution(16923632501110698445)
XLA Ops:
  0.7 1.3 jit_solution_.3.freq
  1.9 572.2 %layers.1 = (bf16[1024,2048]{1,0:T(8,128)(2,1)}, bf16[64,3,8,256,256]{4,3,2,1,0:T(8,128)(2,1)}, bf16[2,8,256,768]{3,2,1,0:T(8,128)(2,1)}) custom-call(bf16[1024,2048]{1,0:T(8,128)(2,1)} %bitcast.4, s32[1]{0:T(128)S(6)} %copy.14.lens, f32[8,128]{1,0:T(8,128)} %jit_solution_.3.freq, f32[2,4,256]{2,1,0:T(4,128)} %ln_own.1, bf16[2,768]{1,0:T(2,128)(2,1)} %bq_own.1, ...), custom_call_target="tpu_custom_call" | custom-call | tf_op jit(solution)/shard_map/layers/pallas_call | solution.py:488
  574.1 4.8 copy.15

commit v3 on v2

--- a/solution.py
+++ b/solution.py
@@ -14,17 +14,21 @@
 SLOTS = 16
 LATE = 4
 ROWS = 256
+DOT_ROWS = 256
 F32 = jnp.float32
 BF16 = jnp.bfloat16
 
 
 def rope_row(rot_dim, width):
     inv_freq = np.float32(1.0) / (np.float32(ROPE_BASE) ** (np.arange(0, rot_dim, 2, dtype=np.float32) / np.float32(rot_dim)))
-    row = np.concatenate([inv_freq, inv_freq, np.zeros(width - rot_dim, np.float32)])
-    return np.broadcast_to(row.astype(np.float32), (8, width))
-
-
-def kernel(dims, hid, lens, freq, ln_own, bq_own, bo_own, bu_own, bd_own, wq_raw, wo, wu, wd, out, gath, wq, xs, a_s, m_s, ctx,
+    lane = lax.broadcasted_iota(jnp.int32, (1, width), 1)
+    row = jnp.zeros((1, width), F32)
+    for i, value in enumerate(inv_freq):
+        row = jnp.where((lane == i) | (lane == i + rot_dim // 2), float(value), row)
+    return row
+
+
+def kernel(dims, hid, lens, ln_own, bq_own, bo_own, bu_own, bd_own, wq_raw, wo, wu, wd, xs, gath, wq, a_s, m_s, ctx,
            act, acc, q_s, k_s, v_s, wbuf, tabs, ln_g, bq_g, bo_g, bu_g, bd_g, bias, raw, raw32, turned, send, rs, ls, ysem, dd,
            ld, small_send, small_recv, raw_in, raw_out, io_sem):
     n, num_layers, heads, tile, seq, d_model, rps, rot_half = dims
@@ -202,24 +206,26 @@
         within(t - 7, wait_sent)
         within(t, own_first)
         within(t - 2, from_sides_again)
-        within(t - 4, wait_sib)
-        within(t - 4, load)
 
     def part1(t):
         within(t - 1, from_sides)
+        within(t - 2, from_far)
         within(t - 3, from_mate(1, right))
+        within(t - 3, from_mate(2, far))
 
     def part2(t):
         within(t, own_second)
-        within(t - 2, from_far)
         within(t - 2, from_mate(0, left))
-        within(t - 3, from_mate(2, far))
+        within(t - 3, wait_sib)
+        within(t - 3, load)
 
     blocks = seq // ROWS
 
     def rows_of(b):
         return pl.ds(b * ROWS, ROWS)
 
+    dot_blocks = [pl.ds(b * DOT_ROWS, DOT_ROWS) for b in range(seq // DOT_ROWS)]
+
     def cols_of(j):
         return pl.ds(pl.multiple_of(j * tile, tile), tile)
 
@@ -229,8 +235,10 @@
     def ln_row(s, l, i):
         return ln_g[s, l, pl.ds(i, 1), :]
 
-    def layer_norms(l):
-        step = 128
+    norm_rows = 128
+
+    def layer_norms(l, first, last):
+        step = norm_rows
 
         def body(b, carry):
             rows = pl.ds(pl.multiple_of(b * step, step), step)
@@ -245,7 +253,7 @@
                 acc[rows, cols] = v[:, s * tile:(s + 1) * tile] + (row(s, l, 3) + row(s, l, 4 + rps))
             return carry
 
-        lax.fori_loop(0, seq // step, body, 0)
+        lax.fori_loop(first, last, body, 0)
 
     def dot(lhs, slot, to):
         return jnp.dot(lhs, wbuf[slot, to], preferred_element_type=F32)
@@ -257,13 +265,13 @@
         return turned.astype(BF16)
 
     def project(l, h, slot, i, ref):
-        for b in range(blocks):
-            v = (dot(a_s[rows_of(b), :], slot, i) + row(h, l, i)).astype(BF16)
+        for rows in dot_blocks:
+            v = (dot(a_s[rows, :], slot, i) + row(h, l, i)).astype(BF16)
             if i < 2:
-                ref[rows_of(b), pl.ds(0, wide)] = rotate(v, rows_of(b))
-                ref[rows_of(b), pl.ds(wide, tile - wide)] = v[:, wide:]
+                ref[rows, pl.ds(0, wide)] = rotate(v, rows)
+                ref[rows, pl.ds(wide, tile - wide)] = v[:, wide:]
             else:
-                ref[rows_of(b), :] = v
+                ref[rows, :] = v
 
     def attend(h, b):
         width = (b + 1) * ROWS
@@ -278,14 +286,14 @@
 
     def up(l, u, slot, to):
         s, rp = u % n, u // n
-        for b in range(blocks):
-            v = dot(m_s[rows_of(b), :], slot, to) + row(s, l, 4 + rp)
+        for rows in dot_blocks:
+            v = dot(m_s[rows, :], slot, to) + row(s, l, 4 + rp)
             g = (0.5 * v) * (1.0 + lax.erf(v * (0.5 ** 0.5)))
-            act[rp, rows_of(b), cols_of(s)] = g.astype(BF16)
+            act[rp, rows, cols_of(s)] = g.astype(BF16)
 
     def add_to(j, slot, to, lhs):
-        for b in range(blocks):
-            acc[rows_of(b), cols_of(j)] += dot(lhs(rows_of(b)), slot, to)
+        for rows in dot_blocks:
+            acc[rows, cols_of(j)] += dot(lhs(rows), slot, to)
 
     def down(v, slot, to):
         add_to(v % n_c, slot, to, lambda rows: act[v // n_c, rows, :])
@@ -293,30 +301,30 @@
     def head_step(l, h):
         k = l * per_layer + n_b + h
         slot = k % 2
-        part1(k + 4)
+        part0(k + 4)
         loaded(slot, 0)
         loaded(slot, 1)
         project(l, h, slot, 0, q_s)
         project(l, h, slot, 1, k_s)
-        part2(k + 4)
+        part1(k + 4)
         loaded(slot, 2)
         project(l, h, slot, 2, v_s)
         for b in range(blocks // 2):
             attend(h, b)
-        part0(k + 5)
+        part2(k + 4)
         for b in range(blocks // 2, blocks):
             attend(h, b)
 
     def up_step(l, j):
         k = l * per_layer + j
         slot = k % 2
-        part1(k + 4)
+        part0(k + 4)
         loaded(slot, 0)
         up(l, 2 * j, slot, 0)
-        part2(k + 4)
+        part1(k + 4)
         loaded(slot, 2)
         up(l, 2 * j + 1, slot, 2)
-        part0(k + 5)
+        part2(k + 4)
 
         @pl.when(j >= LATE)
         def _():
@@ -326,7 +334,7 @@
     def down_step(l, j):
         k = l * per_layer + n_a + n_b + j
         slot = k % 2
-        part1(k + 4)
+        part0(k + 4)
         loaded(slot, 0)
         down(n_b + 2 * j, slot, 0)
 
@@ -335,18 +343,19 @@
             loaded(slot, 3)
             down(n_b - LATE + j, slot, 3)
 
-        part2(k + 4)
+        part1(k + 4)
         loaded(slot, 2)
         down(n_b + 2 * j + 1, slot, 2)
-        part0(k + 5)
+        part2(k + 4)
         loaded(slot, 1)
         add_to(j, slot, 1, lambda rows: ctx[rows, :])
 
     def rotary_tables():
+        freq = rope_row(2 * rot_half, wide)
         for b in range(blocks):
             at = (lax.broadcasted_iota(jnp.int32, (ROWS, wide), 0) + b * ROWS).astype(F32)
             lane = lax.broadcasted_iota(jnp.int32, (ROWS, wide), 1)
-            angle = at * freq[0:1, :]
+            angle = at * freq
             cos, sin = jnp.cos(angle), jnp.sin(angle)
             tabs[0, rows_of(b), :] = jnp.where(lane < 2 * rot_half, cos, 1.0)
             tabs[1, rows_of(b), :] = jnp.where(lane < rot_half, -sin, 0.0)
@@ -408,13 +417,14 @@
     pl.semaphore_signal(barrier, inc=1, device_id=to_mate, device_id_type=MESH)
     pl.semaphore_wait(barrier, n)
 
-    own_first(0)
-    own_second(0)
-    part0(1)
     smalls = ((ln_own, ln_g), (bq_own, bq_g), (bo_own, bo_g), (bu_own, bu_g), (bd_own, bd_g))
     for i, (own, everyone) in enumerate(smalls):
         for step in range(1, n):
             remote(own, everyone.at[f], small_send.at[i], small_recv.at[i], {"fsdp": (f + step) % n}).start()
+    own_first(0)
+    own_second(0)
+    part0(1)
+    for own, everyone in smalls:
         everyone[f] = own[...]
     rotary_tables()
     part1(1)
@@ -425,14 +435,17 @@
     unpack_biases()
     part2(1)
     get_hidden.wait()
-    layer_norms(0)
-    cuts = [raws * i // 6 for i in range(7)]
-    for i, (part, t) in enumerate(((part0, 2), (part1, 2), (part2, 2), (part0, 3), (part1, 3), (part2, 3))):
-        part(t)
-        by_head(cuts[i], cuts[i + 1])
+    norms = seq // norm_rows
+    for i, part in enumerate((part0, part1, part2, part0)):
+        layer_norms(0, norms * i // 4, norms * (i + 1) // 4)
+        part(2 + i // 3)
+    by_head(0, raws // 3)
+    part1(3)
+    by_head(raws // 3, raws * 2 // 3)
+    part2(3)
+    by_head(raws * 2 // 3, raws)
     put_raw(raws - 2).wait()
     put_raw(raws - 1).wait()
-    part0(4)
 
     def layer(l, carry):
         def loop(count, step):
@@ -444,7 +457,7 @@
 
         @pl.when(l > 0)
         def _():
-            layer_norms(l)
+            layer_norms(l, 0, seq // norm_rows)
 
         loop(n_b, up_step)
         loop(n_a, head_step)
@@ -454,11 +467,8 @@
         return carry
 
     lax.fori_loop(0, num_layers, layer, 0)
-    put = pltpu.make_async_copy(xs, out, io_sem)
-    put.start()
-    wait_sent(chunks - 2)
-    wait_sent(chunks - 1)
-    put.wait()
+    for k in range(chunks - 3, chunks):
+        wait_sent(k)
 
 
 def solution(mesh):
@@ -488,13 +498,12 @@
         out, _, _ = pl.pallas_call(
             functools.partial(kernel, dims),
             name="layers",
-            out_shape=(jax.ShapeDtypeStruct((seq, d_model), BF16),
+            out_shape=(pltpu.VMEM((seq, d_model), BF16),
                        jax.ShapeDtypeStruct((chunks, 3, n, tile, tile), BF16),
                        jax.ShapeDtypeStruct((num_layers, heads, tile, triple), BF16)),
-            in_specs=[anywhere, pl.BlockSpec(memory_space=pltpu.SMEM), vmem] + [vmem] * 5 + [anywhere] * 4,
-            out_specs=(anywhere, anywhere, anywhere),
+            in_specs=[anywhere, pl.BlockSpec(memory_space=pltpu.SMEM)] + [vmem] * 5 + [anywhere] * 4,
+            out_specs=(vmem, anywhere, anywhere),
             scratch_shapes=[
-                pltpu.VMEM((seq, d_model), BF16),
                 pltpu.VMEM((seq, d_model), BF16),
                 pltpu.VMEM((seq, d_model), BF16),
                 pltpu.VMEM((seq, d_model), BF16),
@@ -523,8 +532,8 @@
                 dma,
             ],
             compiler_params=pltpu.CompilerParams(
-                collective_id=0, has_side_effects=True, vmem_limit_bytes=67043328),
-        )(hidden.reshape(seq, d_model), lens, jnp.asarray(rope_row(2 * rot_half, wide)), *smalls,
+                collective_id=0, has_side_effects=True, vmem_limit_bytes=59 * 2**20),
+        )(hidden.reshape(seq, d_model), lens, *smalls,
           w_qkv.reshape(num_layers, tile * heads, triple), w_out, w_up, w_down)
         return out.reshape(1, seq, d_model)
 

time: 580 us -> 571 us (0.984)
  no operation moved by 1% of the time
where the time goes in v3:
time: 571 us; the launch traced here: 570 us
  Pallas kernels  568 us (99%)
    pallas_call x1, Pallas kernels, local_step(): pl.pallas_call(functools.partial(kernel, dims), name='layers', out_shape=...  568 us

profile of v3, /device:TPU:113, one launch (start us, length us, event | category | flops | bytes accessed | tf_op | source)
XLA Modules:
  0.0 570.4 jit_solution(10925909949147983206)
XLA Ops:
  0.7 567.7 %layers.1 = (bf16[1024,2048]{1,0:T(8,128)(2,1)S(1)}, bf16[64,3,8,256,256]{4,3,2,1,0:T(8,128)(2,1)}, bf16[2,8,256,768]{3,2,1,0:T(8,128)(2,1)}) custom-call(bf16[1024,2048]{1,0:T(8,128)(2,1)} %bitcast.5, s32[1]{0:T(128)S(6)} %copy.14.lens, f32[2,4,256]{2,1,0:T(4,128)} %ln_own.1, bf16[2,768]{1,0:T(2,128)(2,1)} %bq_own.1, bf16[2,256]{1,0:T(2,128)(2,1)} %bo_own.1, ...), custom_call_target="tpu_custom_call" | custom-call | tf_op jit(solution)/shard_map/layers/pallas_call | solution.py:498
  568.4 2.0 copy.13

commit v4 on v3

--- a/solution.py
+++ b/solution.py
@@ -12,6 +12,7 @@
 LN_EPS = 1e-5
 MESH = pl.DeviceIdType.MESH
 SLOTS = 16
+AHEAD = 1
 LATE = 4
 ROWS = 256
 DOT_ROWS = 256
@@ -90,8 +91,8 @@
         def go(own):
             remote(own(mine), gath.at[k, mine, f], send.at[slot], rs.at[slot, 0], to_right).start()
             remote(own(1), gath.at[k, 1, f], send.at[slot], ls.at[slot, 0], to_left).start()
-            for i in (mine, 1):
-                remote(own(i), gath.at[k, i, f], send.at[slot], dd.at[slot], to_sib).start()
+            for role, i in enumerate((mine, 1)):
+                remote(own(i), gath.at[k, i, f], send.at[slot], dd.at[slot, role], to_sib).start()
 
         with_own(k, go)
 
@@ -101,7 +102,7 @@
         def go(own):
             remote(own(1), gath.at[k, 1, f], send.at[slot], rs.at[slot, 1], to_right).start()
             remote(own(mine), gath.at[k, mine, f], send.at[slot], ls.at[slot, 1], to_left).start()
-            remote(own(other), gath.at[k, other, f], send.at[slot], dd.at[slot], to_sib).start()
+            remote(own(other), gath.at[k, other, f], send.at[slot], dd.at[slot, 2], to_sib).start()
 
         with_own(k, go)
 
@@ -118,41 +119,40 @@
         wait_tile(rs.at[slot, 0])
         pass_on(k, mine, left, rs.at[slot, 2], to_right)
         pass_on(k, mine, left, ysem.at[slot, 0], to_mate)
-        pass_on(k, mine, left, dd.at[slot], to_sib)
+        pass_on(k, mine, left, dd.at[slot, 0], to_sib)
         wait_tile(ls.at[slot, 0])
         pass_on(k, 1, right, ls.at[slot, 2], to_left)
-        pass_on(k, 1, right, dd.at[slot], to_sib)
+        pass_on(k, 1, right, dd.at[slot, 1], to_sib)
 
     def from_sides_again(k):
         slot = k % SLOTS
         wait_tile(ls.at[slot, 1])
         pass_on(k, mine, right, ysem.at[slot, 1], to_mate)
-        pass_on(k, mine, right, dd.at[slot], to_sib)
+        pass_on(k, mine, right, dd.at[slot, 0], to_sib)
         wait_tile(rs.at[slot, 1])
-        pass_on(k, 1, left, dd.at[slot], to_sib)
+        pass_on(k, 1, left, dd.at[slot, 1], to_sib)
 
     def from_far(k):
         slot = k % SLOTS
         wait_tile(rs.at[slot, 2])
         pass_on(k, mine, far, ysem.at[slot, 2], to_mate)
-        pass_on(k, mine, far, dd.at[slot], to_sib)
+        pass_on(k, mine, far, dd.at[slot, 0], to_sib)
         wait_tile(ls.at[slot, 2])
-        pass_on(k, 1, far, dd.at[slot], to_sib)
+        pass_on(k, 1, far, dd.at[slot, 1], to_sib)
 
     def from_mate(i, s):
         def do(k):
             slot = k % SLOTS
             wait_tile(ysem.at[slot, i])
-            pass_on(k, other, s, dd.at[slot], to_sib)
+            pass_on(k, other, s, dd.at[slot, 2], to_sib)
 
         return do
 
-    sib_tiles = 3 * ring
-    sent_tiles = 3 * (ring - 1) + sib_tiles
-
-    def wait_sib(k):
-        ref = gath.at[0, :, pl.ds(0, sib_tiles // 3)]
-        pltpu.make_async_copy(ref, ref, dd.at[k % SLOTS]).wait()
+    sent_tiles = 3 * (ring - 1) + 3 * ring
+
+    def wait_sib(k, role):
+        ref = gath.at[0, 0, pl.ds(0, ring)]
+        pltpu.make_async_copy(ref, ref, dd.at[k % SLOTS, role]).wait()
 
     def wait_sent(k):
         ref = gath.at[0, :, pl.ds(0, sent_tiles // 3)]
@@ -166,7 +166,18 @@
                 gath.at[kk, i, s], wbuf.at[slot, to, pl.ds(pl.multiple_of(s * tile, tile), tile)], ld.at[slot, to]).start()
         pltpu.make_async_copy(own, wbuf.at[slot, to, pl.ds(pl.multiple_of(f * tile, tile), tile)], ld.at[slot, to]).start()
 
+    def load_down(k, i):
+        j = k % per_layer - n_a - n_b
+        load_tile(k, k, i, i, down_tile(k // per_layer, n_b + 2 * j + i // 2))
+
     def load(k):
+        wait_sib(k, 0)
+        wait_sib(k, 1)
+
+        @pl.when(k < chunks - 1)
+        def _():
+            wait_sib(k, 2)
+
         l, r = k // per_layer, k % per_layer
         j = r - n_a - n_b
 
@@ -186,9 +197,12 @@
 
         @pl.when(r >= n_a + n_b)
         def _():
-            load_tile(k, k, 0, 0, down_tile(l, n_b + 2 * j))
             load_tile(k, k, 1, 1, out_tile(l, j))
-            load_tile(k, k, 2, 2, down_tile(l, n_b + 2 * j + 1))
+            load_down(k, mine)
+
+        @pl.when((r >= n_a + n_b) & (k < chunks - 1))
+        def _():
+            load_down(k, other)
 
         @pl.when((r >= n_a + n_b) & (j < LATE))
         def _():
@@ -197,26 +211,25 @@
     def loaded(slot, to):
         pltpu.make_async_copy(wbuf.at[slot, to], wbuf.at[slot, to], ld.at[slot, to]).wait()
 
-    def within(k, do):
-        @pl.when((k >= 0) & (k < chunks))
+    def within(k, do, end=chunks):
+        @pl.when((k >= 0) & (k < end))
         def _():
             do(k)
 
     def part0(t):
         within(t - 7, wait_sent)
-        within(t, own_first)
+        within(t + AHEAD, own_first)
         within(t - 2, from_sides_again)
 
     def part1(t):
         within(t - 1, from_sides)
         within(t - 2, from_far)
         within(t - 3, from_mate(1, right))
-        within(t - 3, from_mate(2, far))
+        within(t - 3, from_mate(2, far), chunks - 1)
 
     def part2(t):
-        within(t, own_second)
+        within(t + AHEAD, own_second)
         within(t - 2, from_mate(0, left))
-        within(t - 3, wait_sib)
         within(t - 3, load)
 
     blocks = seq // ROWS
@@ -335,8 +348,8 @@
         k = l * per_layer + n_a + n_b + j
         slot = k % 2
         part0(k + 4)
-        loaded(slot, 0)
-        down(n_b + 2 * j, slot, 0)
+        loaded(slot, 1)
+        add_to(j, slot, 1, lambda rows: ctx[rows, :])
 
         @pl.when(j < LATE)
         def _():
@@ -344,11 +357,24 @@
             down(n_b - LATE + j, slot, 3)
 
         part1(k + 4)
-        loaded(slot, 2)
-        down(n_b + 2 * j + 1, slot, 2)
+        loaded(slot, mine)
+        down(n_b + 2 * j + mine // 2, slot, mine)
         part2(k + 4)
-        loaded(slot, 1)
-        add_to(j, slot, 1, lambda rows: ctx[rows, :])
+
+        @pl.when(k == chunks - 1)
+        def _():
+            from_mate(2, far)(k)
+            wait_sib(k, 2)
+            load_down(k, other)
+
+        loaded(slot, other)
+        down(n_b + 2 * j + other // 2, slot, other)
+
+        @pl.when(j >= n_c // 2)
+        def _():
+            cols = pl.ds(pl.multiple_of((2 * j - n_c) * tile, 2 * tile), 2 * tile)
+            for b in range(blocks):
+                xs[rows_of(b), cols] = acc[rows_of(b), cols].astype(BF16)
 
     def rotary_tables():
         freq = rope_row(2 * rot_half, wide)
@@ -418,11 +444,13 @@
     pl.semaphore_wait(barrier, n)
 
     smalls = ((ln_own, ln_g), (bq_own, bq_g), (bo_own, bo_g), (bu_own, bu_g), (bd_own, bd_g))
+    own_first(0)
     for i, (own, everyone) in enumerate(smalls):
         for step in range(1, n):
             remote(own, everyone.at[f], small_send.at[i], small_recv.at[i], {"fsdp": (f + step) % n}).start()
-    own_first(0)
     own_second(0)
+    part0(0)
+    part2(0)
     part0(1)
     for own, everyone in smalls:
         everyone[f] = own[...]
@@ -462,8 +490,6 @@
         loop(n_b, up_step)
         loop(n_a, head_step)
         loop(n_c, down_step)
-        for b in range(blocks):
-            xs[rows_of(b), :] = acc[rows_of(b), :].astype(BF16)
         return carry
 
     lax.fori_loop(0, num_layers, layer, 0)
@@ -523,7 +549,7 @@
                 dma((SLOTS, 3)),
                 dma((SLOTS, 3)),
                 dma((SLOTS, 3)),
-                dma((SLOTS,)),
+                dma((SLOTS, 3)),
                 dma((2, 4)),
                 dma((5,)),
                 dma((5,)),

time: 571 us -> 579 us (1.014)
  Pallas kernels: 568 us -> 576 us
    pallas_call x1, Pallas kernels: 568 us -> 576 us  [local_step(): pl.pallas_call(functools.partial(kernel, dims), name='layers', out_shape=...]
where the time goes in v4:
time: 579 us; the launch traced here: 578 us
  Pallas kernels  576 us (99%)
    pallas_call x1, Pallas kernels, local_step(): pl.pallas_call(functools.partial(kernel, dims), name='layers', out_shape=...  576 us

profile of v4, /device:TPU:113, one launch (start us, length us, event | category | flops | bytes accessed | tf_op | source)
XLA Modules:
  0.0 578.2 jit_solution(4078983178775921153)
XLA Ops:
  0.7 575.5 %layers.1 = (bf16[1024,2048]{1,0:T(8,128)(2,1)S(1)}, bf16[64,3,8,256,256]{4,3,2,1,0:T(8,128)(2,1)}, bf16[2,8,256,768]{3,2,1,0:T(8,128)(2,1)}) custom-call(bf16[1024,2048]{1,0:T(8,128)(2,1)} %bitcast.5, s32[1]{0:T(128)S(6)} %copy.14.lens, f32[2,4,256]{2,1,0:T(4,128)} %ln_own.1, bf16[2,768]{1,0:T(2,128)(2,1)} %bq_own.1, bf16[2,256]{1,0:T(2,128)(2,1)} %bo_own.1, ...), custom_call_target="tpu_custom_call" | custom-call | tf_op jit(solution)/shard_map/layers/pallas_call | solution.py:524
  576.2 2.0 copy.13

commit v5 on v4

--- a/solution.py
+++ b/solution.py
@@ -12,7 +12,6 @@
 LN_EPS = 1e-5
 MESH = pl.DeviceIdType.MESH
 SLOTS = 16
-AHEAD = 1
 LATE = 4
 ROWS = 256
 DOT_ROWS = 256
@@ -171,15 +170,9 @@
         load_tile(k, k, i, i, down_tile(k // per_layer, n_b + 2 * j + i // 2))
 
     def load(k):
-        wait_sib(k, 0)
-        wait_sib(k, 1)
-
-        @pl.when(k < chunks - 1)
-        def _():
-            wait_sib(k, 2)
-
         l, r = k // per_layer, k % per_layer
-        j = r - n_a - n_b
+        for role in range(3):
+            wait_sib(k, role)
 
         @pl.when(r < n_b)
         def _():
@@ -190,47 +183,55 @@
         def _():
             load_tile(k, k - LATE, 1, 3, down_tile(l, r - LATE))
 
-        @pl.when((r >= n_b) & (r < n_b + n_a))
+        @pl.when(r >= n_b)
         def _():
             for i in range(3):
                 load_tile(k, k, i, i, q_tile(l, r - n_b, i))
 
-        @pl.when(r >= n_a + n_b)
-        def _():
-            load_tile(k, k, 1, 1, out_tile(l, j))
-            load_down(k, mine)
-
-        @pl.when((r >= n_a + n_b) & (k < chunks - 1))
-        def _():
-            load_down(k, other)
-
-        @pl.when((r >= n_a + n_b) & (j < LATE))
+    def load_first(k):
+        l, j = k // per_layer, k % per_layer - n_a - n_b
+        for role in range(2):
+            wait_sib(k, role)
+        load_tile(k, k, 1, 1, out_tile(l, j))
+        load_down(k, mine)
+
+        @pl.when(j < LATE)
         def _():
             load_tile(k, k - n_a - LATE, 1, 3, down_tile(l, n_b - LATE + j))
+
+    def load_last(k):
+        wait_sib(k, 2)
+        load_down(k, other)
 
     def loaded(slot, to):
         pltpu.make_async_copy(wbuf.at[slot, to], wbuf.at[slot, to], ld.at[slot, to]).wait()
 
-    def within(k, do, end=chunks):
-        @pl.when((k >= 0) & (k < end))
+    def within(k, do, phases=None):
+        r = k % per_layer
+        these = {None: True, "first": r < n_a + n_b, "last": r >= n_a + n_b}[phases]
+
+        @pl.when((k >= 0) & (k < chunks) & these)
         def _():
             do(k)
 
     def part0(t):
         within(t - 7, wait_sent)
-        within(t + AHEAD, own_first)
-        within(t - 2, from_sides_again)
+        within(t, own_first)
+        within(t - 1, from_sides)
+        within(t - 4, from_mate(2, far), "last")
 
     def part1(t):
-        within(t - 1, from_sides)
         within(t - 2, from_far)
         within(t - 3, from_mate(1, right))
-        within(t - 3, from_mate(2, far), chunks - 1)
+        within(t - 3, from_mate(2, far), "first")
+        within(t - 4, load_last, "last")
 
     def part2(t):
-        within(t + AHEAD, own_second)
+        within(t, own_second)
+        within(t - 1, from_sides_again)
         within(t - 2, from_mate(0, left))
-        within(t - 3, load)
+        within(t - 2, load_first, "last")
+        within(t - 3, load, "first")
 
     blocks = seq // ROWS
 
@@ -328,6 +329,10 @@
         for b in range(blocks // 2, blocks):
             attend(h, b)
 
+        @pl.when(h == n_a - 1)
+        def _():
+            out_now(0, 1 - slot)
+
     def up_step(l, j):
         k = l * per_layer + j
         slot = k % 2
@@ -344,31 +349,40 @@
             loaded(slot, 3)
             down(j - LATE, slot, 3)
 
+    def out_now(j, slot):
+        loaded(slot, 1)
+        add_to(j, slot, 1, lambda rows: ctx[rows, :])
+
+    def down_now(j, slot, i):
+        loaded(slot, i)
+        down(n_b + 2 * j + i // 2, slot, i)
+
     def down_step(l, j):
         k = l * per_layer + n_a + n_b + j
         slot = k % 2
         part0(k + 4)
-        loaded(slot, 1)
-        add_to(j, slot, 1, lambda rows: ctx[rows, :])
+
+        @pl.when(j == 0)
+        def _():
+            down_now(j, slot, mine)
+
+        @pl.when(j < n_c - 1)
+        def _():
+            out_now(j + 1, 1 - slot)
+
+        part1(k + 4)
+
+        @pl.when(j < n_c - 1)
+        def _():
+            down_now(j + 1, 1 - slot, mine)
 
         @pl.when(j < LATE)
         def _():
             loaded(slot, 3)
             down(n_b - LATE + j, slot, 3)
 
-        part1(k + 4)
-        loaded(slot, mine)
-        down(n_b + 2 * j + mine // 2, slot, mine)
         part2(k + 4)
-
-        @pl.when(k == chunks - 1)
-        def _():
-            from_mate(2, far)(k)
-            wait_sib(k, 2)
-            load_down(k, other)
-
-        loaded(slot, other)
-        down(n_b + 2 * j + other // 2, slot, other)
+        down_now(j, slot, other)
 
         @pl.when(j >= n_c // 2)
         def _():
@@ -449,18 +463,16 @@
         for step in range(1, n):
             remote(own, everyone.at[f], small_send.at[i], small_recv.at[i], {"fsdp": (f + step) % n}).start()
     own_second(0)
-    part0(0)
-    part2(0)
-    part0(1)
     for own, everyone in smalls:
         everyone[f] = own[...]
     rotary_tables()
-    part1(1)
+    part0(1)
     for i, (own, everyone) in enumerate(smalls):
         ref = everyone.at[pl.ds(0, n - 1)]
         pltpu.make_async_copy(ref, ref, small_send.at[i]).wait()
         pltpu.make_async_copy(ref, ref, small_recv.at[i]).wait()
     unpack_biases()
+    part1(1)
     part2(1)
     get_hidden.wait()
     norms = seq // norm_rows

time: 579 us -> 567 us (0.979)
  Pallas kernels: 576 us -> 564 us
    pallas_call x1, Pallas kernels: 576 us -> 564 us  [local_step(): pl.pallas_call(functools.partial(kernel, dims), name='layers', out_shape=...]
where the time goes in v5:
time: 567 us; the launch traced here: 566 us
  Pallas kernels  564 us (99%)
    pallas_call x1, Pallas kernels, local_step(): pl.pallas_call(functools.partial(kernel, dims), name='layers', out_shape=...  564 us

profile of v5, /device:TPU:113, one launch (start us, length us, event | category | flops | bytes accessed | tf_op | source)
XLA Modules:
  0.0 566.3 jit_solution(3607119988857912911)
XLA Ops:
  0.7 563.6 %layers.1 = (bf16[1024,2048]{1,0:T(8,128)(2,1)S(1)}, bf16[64,3,8,256,256]{4,3,2,1,0:T(8,128)(2,1)}, bf16[2,8,256,768]{3,2,1,0:T(8,128)(2,1)}) custom-call(bf16[1024,2048]{1,0:T(8,128)(2,1)} %bitcast.5, s32[1]{0:T(128)S(6)} %copy.14.lens, f32[2,4,256]{2,1,0:T(4,128)} %ln_own.1, bf16[2,768]{1,0:T(2,128)(2,1)} %bq_own.1, bf16[2,256]{1,0:T(2,128)(2,1)} %bo_own.1, ...), custom_call_target="tpu_custom_call" | custom-call | tf_op jit(solution)/shard_map/layers/pallas_call | solution.py:536
  564.3 2.0 copy.13

commit v6 on v5

--- a/solution.py
+++ b/solution.py
@@ -28,9 +28,9 @@
     return row
 
 
-def kernel(dims, hid, lens, ln_own, bq_own, bo_own, bu_own, bd_own, wq_raw, wo, wu, wd, xs, gath, wq, a_s, m_s, ctx,
-           act, acc, q_s, k_s, v_s, wbuf, tabs, ln_g, bq_g, bo_g, bu_g, bd_g, bias, raw, raw32, turned, send, rs, ls, ysem, dd,
-           ld, small_send, small_recv, raw_in, raw_out, io_sem):
+def kernel(dims, hid, lens_own, ln_own, bq_own, bo_own, bu_own, bd_own, wq_raw, wo, wu, wd, xs, gath, wq, a_s, m_s, ctx,
+           act, acc, q_s, k_s, v_s, wbuf, tabs, lens, ln_g, bq_g, bo_g, bu_g, bd_g, bias, raw, raw32, turned, send, rs, ls, ysem, dd,
+           ld, small_send, small_recv, small_own, raw_in, raw_out, io_sem):
     n, num_layers, heads, tile, seq, d_model, rps, rot_half = dims
     ring = n // 2
     n_a, n_b, n_c = heads, n * rps // 2, d_model // tile
@@ -86,10 +86,14 @@
 
     def own_first(k):
         slot = k % SLOTS
+        at_once = isinstance(k, int)
 
         def go(own):
             remote(own(mine), gath.at[k, mine, f], send.at[slot], rs.at[slot, 0], to_right).start()
-            remote(own(1), gath.at[k, 1, f], send.at[slot], ls.at[slot, 0], to_left).start()
+            if at_once:
+                remote(own(mine), gath.at[k, mine, f], send.at[slot], ls.at[slot, 1], to_left).start()
+            else:
+                remote(own(1), gath.at[k, 1, f], send.at[slot], ls.at[slot, 0], to_left).start()
             for role, i in enumerate((mine, 1)):
                 remote(own(i), gath.at[k, i, f], send.at[slot], dd.at[slot, role], to_sib).start()
 
@@ -97,10 +101,14 @@
 
     def own_second(k):
         slot = k % SLOTS
+        at_once = isinstance(k, int)
 
         def go(own):
             remote(own(1), gath.at[k, 1, f], send.at[slot], rs.at[slot, 1], to_right).start()
-            remote(own(mine), gath.at[k, mine, f], send.at[slot], ls.at[slot, 1], to_left).start()
+            if at_once:
+                remote(own(1), gath.at[k, 1, f], send.at[slot], ls.at[slot, 0], to_left).start()
+            else:
+                remote(own(mine), gath.at[k, mine, f], send.at[slot], ls.at[slot, 1], to_left).start()
             remote(own(other), gath.at[k, other, f], send.at[slot], dd.at[slot, 2], to_sib).start()
 
         with_own(k, go)
@@ -113,23 +121,37 @@
         t = gath.at[k, i, s]
         remote(t, t, send.at[k % SLOTS], sem, where).start()
 
-    def from_sides(k):
+    def left_mine(k):
         slot = k % SLOTS
         wait_tile(rs.at[slot, 0])
         pass_on(k, mine, left, rs.at[slot, 2], to_right)
         pass_on(k, mine, left, ysem.at[slot, 0], to_mate)
         pass_on(k, mine, left, dd.at[slot, 0], to_sib)
+
+    def right_one(k):
+        slot = k % SLOTS
         wait_tile(ls.at[slot, 0])
         pass_on(k, 1, right, ls.at[slot, 2], to_left)
         pass_on(k, 1, right, dd.at[slot, 1], to_sib)
 
-    def from_sides_again(k):
+    def right_mine(k):
         slot = k % SLOTS
         wait_tile(ls.at[slot, 1])
         pass_on(k, mine, right, ysem.at[slot, 1], to_mate)
         pass_on(k, mine, right, dd.at[slot, 0], to_sib)
+
+    def left_one(k):
+        slot = k % SLOTS
         wait_tile(rs.at[slot, 1])
         pass_on(k, 1, left, dd.at[slot, 1], to_sib)
+
+    def from_sides(k):
+        left_mine(k)
+        right_one(k)
+
+    def from_sides_again(k):
+        right_mine(k)
+        left_one(k)
 
     def from_far(k):
         slot = k % SLOTS
@@ -336,7 +358,11 @@
     def up_step(l, j):
         k = l * per_layer + j
         slot = k % 2
-        part0(k + 4)
+
+        @pl.when((l == 0) | (j > 0))
+        def _():
+            part0(k + 4)
+
         loaded(slot, 0)
         up(l, 2 * j, slot, 0)
         part1(k + 4)
@@ -463,26 +489,33 @@
         for step in range(1, n):
             remote(own, everyone.at[f], small_send.at[i], small_recv.at[i], {"fsdp": (f + step) % n}).start()
     own_second(0)
-    for own, everyone in smalls:
-        everyone[f] = own[...]
+    mine_too = [pltpu.make_async_copy(own, everyone.at[f], small_own.at[i]) for i, (own, everyone) in enumerate(smalls)]
+    mine_too.append(pltpu.make_async_copy(lens_own, lens, small_own.at[len(smalls)]))
+    for copy in mine_too:
+        copy.start()
     rotary_tables()
-    part0(1)
+    own_first(jnp.int32(1))
+    left_mine(0)
+    right_mine(0)
     for i, (own, everyone) in enumerate(smalls):
         ref = everyone.at[pl.ds(0, n - 1)]
         pltpu.make_async_copy(ref, ref, small_send.at[i]).wait()
         pltpu.make_async_copy(ref, ref, small_recv.at[i]).wait()
+    for copy in mine_too:
+        copy.wait()
     unpack_biases()
-    part1(1)
-    part2(1)
+    own_second(jnp.int32(1))
+    right_one(0)
+    left_one(0)
     get_hidden.wait()
     norms = seq // norm_rows
     for i, part in enumerate((part0, part1, part2, part0)):
         layer_norms(0, norms * i // 4, norms * (i + 1) // 4)
-        part(2 + i // 3)
+        part(jnp.int32(2 + i // 3))
     by_head(0, raws // 3)
-    part1(3)
+    part1(jnp.int32(3))
     by_head(raws // 3, raws * 2 // 3)
-    part2(3)
+    part2(jnp.int32(3))
     by_head(raws * 2 // 3, raws)
     put_raw(raws - 2).wait()
     put_raw(raws - 1).wait()
@@ -497,7 +530,9 @@
 
         @pl.when(l > 0)
         def _():
-            layer_norms(l, 0, seq // norm_rows)
+            layer_norms(l, 0, norms // 2)
+            part0(l * per_layer + 4)
+            layer_norms(l, norms // 2, norms)
 
         loop(n_b, up_step)
         loop(n_a, head_step)
@@ -539,7 +574,7 @@
             out_shape=(pltpu.VMEM((seq, d_model), BF16),
                        jax.ShapeDtypeStruct((chunks, 3, n, tile, tile), BF16),
                        jax.ShapeDtypeStruct((num_layers, heads, tile, triple), BF16)),
-            in_specs=[anywhere, pl.BlockSpec(memory_space=pltpu.SMEM)] + [vmem] * 5 + [anywhere] * 4,
+            in_specs=[anywhere] + [pl.BlockSpec(memory_space=pltpu.HBM)] * 6 + [anywhere] * 4,
             out_specs=(vmem, anywhere, anywhere),
             scratch_shapes=[
                 pltpu.VMEM((seq, d_model), BF16),
@@ -552,6 +587,7 @@
                 pltpu.VMEM((seq, tile), BF16),
                 pltpu.VMEM((2, 4, d_model, tile), BF16),
                 pltpu.VMEM((3, seq, wide), F32),
+                pltpu.SMEM(lens.shape, lens.dtype),
                 *[pltpu.VMEM((n,) + p.shape, p.dtype) for p in smalls],
                 pltpu.VMEM((n, num_layers, 16, tile), F32),
                 pltpu.VMEM((2, raw_rows, triple), BF16),
@@ -565,6 +601,7 @@
                 dma((2, 4)),
                 dma((5,)),
                 dma((5,)),
+                dma((6,)),
                 dma((2,)),
                 dma((2,)),
                 dma,

time: 567 us -> 565 us (level)
  no operation moved by 1% of the time
where the time goes in v6:
time: 565 us
  Pallas kernels  562 us (99%)
    pallas_call x1, Pallas kernels, local_step(): pl.pallas_call(functools.partial(kernel, dims), name='layers', out_shape=...  562 us

profile of v6, /device:TPU:113, one launch (start us, length us, event | category | flops | bytes accessed | tf_op | source)
XLA Modules:
  0.0 564.7 jit_solution(15930165845761884172)
XLA Ops:
  0.7 562.0 %layers.1 = (bf16[1024,2048]{1,0:T(8,128)(2,1)S(1)}, bf16[64,3,8,256,256]{4,3,2,1,0:T(8,128)(2,1)}, bf16[2,8,256,768]{3,2,1,0:T(8,128)(2,1)}) custom-call(bf16[1024,2048]{1,0:T(8,128)(2,1)} %bitcast.5, s32[1]{0:T(128)S(6)} %copy.14.lens_own, f32[2,4,256]{2,1,0:T(4,128)} %ln_own.1, bf16[2,768]{1,0:T(2,128)(2,1)} %bq_own.1, bf16[2,256]{1,0:T(2,128)(2,1)} %bo_own.1, ...), custom_call_target="tpu_custom_call" | custom-call | tf_op jit(solution)/shard_map/layers/pallas_call | solution.py:571
  562.7 2.0 copy.13

commit v7 on v6

--- a/solution.py
+++ b/solution.py
@@ -30,7 +30,7 @@
 
 def kernel(dims, hid, lens_own, ln_own, bq_own, bo_own, bu_own, bd_own, wq_raw, wo, wu, wd, xs, gath, wq, a_s, m_s, ctx,
            act, acc, q_s, k_s, v_s, wbuf, tabs, lens, ln_g, bq_g, bo_g, bu_g, bd_g, bias, raw, raw32, turned, send, rs, ls, ysem, dd,
-           ld, small_send, small_recv, small_own, raw_in, raw_out, io_sem):
+           ld, small_send, small_recv, small_own, from_l, from_r, raw_in, raw_out, io_sem):
     n, num_layers, heads, tile, seq, d_model, rps, rot_half = dims
     ring = n // 2
     n_a, n_b, n_c = heads, n * rps // 2, d_model // tile
@@ -53,6 +53,7 @@
         return pltpu.make_async_remote_copy(
             src_ref=src, dst_ref=dst, send_sem=s_sem, recv_sem=r_sem, device_id=where, device_id_type=MESH)
 
+    halves = [pl.ds(i * (tile // 2), tile // 2) for i in range(2)]
     to_right, to_left, to_sib, to_mate = {"fsdp": right}, {"fsdp": left}, {"fsdp": sib}, {"dp": mate}
 
     def q_tile(l, h, i):
@@ -89,10 +90,13 @@
         at_once = isinstance(k, int)
 
         def go(own):
-            remote(own(mine), gath.at[k, mine, f], send.at[slot], rs.at[slot, 0], to_right).start()
             if at_once:
-                remote(own(mine), gath.at[k, mine, f], send.at[slot], ls.at[slot, 1], to_left).start()
+                for half, part in enumerate(halves):
+                    src, dst = own(mine).at[part], gath.at[k, mine, f].at[part]
+                    remote(src, dst, send.at[slot], from_l.at[half], to_right).start()
+                    remote(src, dst, send.at[slot], from_r.at[half], to_left).start()
             else:
+                remote(own(mine), gath.at[k, mine, f], send.at[slot], rs.at[slot, 0], to_right).start()
                 remote(own(1), gath.at[k, 1, f], send.at[slot], ls.at[slot, 0], to_left).start()
             for role, i in enumerate((mine, 1)):
                 remote(own(i), gath.at[k, i, f], send.at[slot], dd.at[slot, role], to_sib).start()
@@ -120,6 +124,17 @@
     def pass_on(k, i, s, sem, where):
         t = gath.at[k, i, s]
         remote(t, t, send.at[k % SLOTS], sem, where).start()
+
+    def both_mine(k):
+        slot = k % SLOTS
+        for half, part in enumerate(halves):
+            for sem, s, onward, i in ((from_l, left, True, 0), (from_r, right, False, 1)):
+                t = gath.at[k, mine, s].at[part]
+                pltpu.make_async_copy(t, t, sem.at[half]).wait()
+                remote(t, t, send.at[slot], ysem.at[slot, i], to_mate).start()
+                if onward:
+                    remote(t, t, send.at[slot], rs.at[slot, 2], to_right).start()
+                remote(t, t, send.at[slot], dd.at[slot, 0], to_sib).start()
 
     def left_mine(k):
         slot = k % SLOTS
@@ -495,8 +510,7 @@
         copy.start()
     rotary_tables()
     own_first(jnp.int32(1))
-    left_mine(0)
-    right_mine(0)
+    both_mine(0)
     for i, (own, everyone) in enumerate(smalls):
         ref = everyone.at[pl.ds(0, n - 1)]
         pltpu.make_async_copy(ref, ref, small_send.at[i]).wait()
@@ -604,6 +618,8 @@
                 dma((6,)),
                 dma((2,)),
                 dma((2,)),
+                dma((2,)),
+                dma((2,)),
                 dma,
             ],
             compiler_params=pltpu.CompilerParams(

time: 565 us -> 565 us (level)
  no operation moved by 1% of the time
where the time goes in v7:
time: 565 us
  Pallas kernels  562 us (99%)
    pallas_call x1, Pallas kernels, local_step(): pl.pallas_call(functools.partial(kernel, dims), name='layers', out_shape=...  562 us

profile of v7, /device:TPU:113, one launch (start us, length us, event | category | flops | bytes accessed | tf_op | source)
XLA Modules:
  0.0 564.7 jit_solution(17717812741901570443)
XLA Ops:
  0.7 562.1 %layers.1 = (bf16[1024,2048]{1,0:T(8,128)(2,1)S(1)}, bf16[64,3,8,256,256]{4,3,2,1,0:T(8,128)(2,1)}, bf16[2,8,256,768]{3,2,1,0:T(8,128)(2,1)}) custom-call(bf16[1024,2048]{1,0:T(8,128)(2,1)} %bitcast.5, s32[1]{0:T(128)S(6)} %copy.14.lens_own, f32[2,4,256]{2,1,0:T(4,128)} %ln_own.1, bf16[2,768]{1,0:T(2,128)(2,1)} %bq_own.1, bf16[2,256]{1,0:T(2,128)(2,1)} %bo_own.1, ...), custom_call_target="tpu_custom_call" | custom-call | tf_op jit(solution)/shard_map/layers/pallas_call | solution.py:585
  562.7 2.0 copy.13
